TPU v7x, 32 devices: a 4x4x1 block of a 4x4x8 slice. The times are simulated.
32 devices in a mesh: rep: 1 (over z), mp: 4 (over y), tb: 4 (over x), ta: 2 (over core).
Axes of the slice: x: 4, y: 4, z: 1, core: 2. Of those that a mesh axis runs over, the one named last changes fastest.
The devices are a block of a 4x4x8 slice.
Arguments:
- x_in: bfloat16 [512, 3072], P(('rep', 'tb', 'ta'), 'mp')
- seg_ids: int32 [512], P(('rep', 'tb', 'ta'))
- pos_ids: int32 [512], P(('rep', 'tb', 'ta'))
- w_q: bfloat16 [2, 3072, 4096], P(None, ('tb', 'ta'), 'mp')
- w_k: bfloat16 [2, 3072, 256], P(None, ('tb', 'ta'))
- w_v: bfloat16 [2, 3072, 256], P(None, ('tb', 'ta'))
- w_gate: bfloat16 [2, 3072, 24576], P(None, ('tb', 'ta'), 'mp')
- w_up: bfloat16 [2, 3072, 24576], P(None, ('tb', 'ta'), 'mp')
- w_out: bfloat16 [2, 4096, 3072], P(None, 'mp', ('tb', 'ta'))
- w_down: bfloat16 [2, 24576, 3072], P(None, 'mp', ('tb', 'ta'))
- norm_gain: bfloat16 [2, 3072], replicated
Outputs:
- output: float32 [512, 3072], P(('rep', 'tb', 'ta'), 'mp')
All inputs are finite; a program needn't handle non-finite values.
Results may differ from a plain program's by a relative error of at most 0.00926904.
Values are sent between devices in bfloat16 or wider.
A program may use at most 768 MiB of HBM per device.

v0:
```python
import jax
import jax.numpy as jnp
from jax import lax
from jax.sharding import PartitionSpec as P

ROPE_BASE = 10000.0
NORM_EPS = 1e-6
TOKEN_AXES = ("rep", "tb", "ta")
PLANE_AXES = ("tb", "ta")


def rope_tables(pos_ids, head_dim):
    half_dim = head_dim // 2
    inv_freq = ROPE_BASE ** (-(jnp.arange(half_dim, dtype=jnp.float32) * 2.0) / head_dim)
    angles = pos_ids.astype(jnp.float32)[:, None] * inv_freq[None, :]
    return jnp.cos(angles), jnp.sin(angles)


def apply_rope(rot_in, cos_tab, sin_tab):
    half_dim = rot_in.shape[-1] // 2
    lower_half = rot_in[..., :half_dim].astype(jnp.float32)
    upper_half = rot_in[..., half_dim:].astype(jnp.float32)
    return jnp.concatenate([lower_half * cos_tab - upper_half * sin_tab, upper_half * cos_tab + lower_half * sin_tab], axis=-1).astype(jnp.bfloat16)


def block_attention(q_rot, k_rot, v_proj, seg_q, pos_q, seg_k, pos_k):
    score_scale = q_rot.shape[-1] ** -0.5
    scores = jnp.einsum("thd,sd->hts", q_rot, k_rot, preferred_element_type=jnp.float32) * score_scale
    allowed = (seg_q[:, None] == seg_k[None, :]) & (pos_k[None, :] <= pos_q[:, None])
    scores = jnp.where(allowed[None], scores, -1e30)
    row_peak = jnp.max(scores, axis=-1, keepdims=True)
    exp_scores = jnp.exp(scores - row_peak)
    prob_bf16 = (exp_scores / jnp.sum(exp_scores, axis=-1, keepdims=True)).astype(jnp.bfloat16)
    return jnp.einsum("hts,sd->thd", prob_bf16, v_proj, preferred_element_type=jnp.float32).astype(jnp.bfloat16)


def solution(mesh):
    mp_size = mesh.shape["mp"]

    def device_body(x_loc, seg_ids, pos_ids, w_q, w_k, w_v, w_gate, w_up, w_out, w_down, gain_loc):
        num_tokens, embed_loc = x_loc.shape
        head_dim = w_k.shape[-1]
        width_q = w_q.shape[-1]
        width_ff = w_gate.shape[-1]
        edge_k = width_q + head_dim
        edge_v = edge_k + head_dim
        edge_g = edge_v + width_ff
        cos_tab, sin_tab = rope_tables(pos_ids, head_dim)
        hidden = x_loc.astype(jnp.float32)
        for layer_idx in range(w_q.shape[0]):
            sq_part = jnp.sum(hidden * hidden, axis=-1, keepdims=True)
            mean_sq = lax.psum(sq_part, "mp") / (embed_loc * mp_size)
            normed_loc = (hidden * lax.rsqrt(mean_sq + NORM_EPS) * gain_loc[layer_idx].astype(jnp.float32)).astype(jnp.bfloat16)
            normed = lax.all_gather(normed_loc, "mp", axis=1, tiled=True)
            w_in_loc = jnp.concatenate([w_q[layer_idx], w_k[layer_idx], w_v[layer_idx], w_gate[layer_idx], w_up[layer_idx]], axis=1)
            w_in = lax.all_gather(w_in_loc, PLANE_AXES, axis=0, tiled=True)
            proj_all = jnp.dot(normed, w_in, preferred_element_type=jnp.float32).astype(jnp.bfloat16)
            q_rot = apply_rope(proj_all[:, :width_q].reshape(num_tokens, width_q // head_dim, head_dim), cos_tab[:, None, :], sin_tab[:, None, :])
            k_rot = apply_rope(proj_all[:, width_q:edge_k], cos_tab, sin_tab)
            attn = block_attention(q_rot, k_rot, proj_all[:, edge_k:edge_v], seg_ids, pos_ids, seg_ids, pos_ids)
            mlp_act = (jax.nn.silu(proj_all[:, edge_v:edge_g].astype(jnp.float32)) * proj_all[:, edge_g:].astype(jnp.float32)).astype(jnp.bfloat16)
            w_back_loc = jnp.concatenate([w_out[layer_idx], w_down[layer_idx]], axis=0)
            w_back = lax.all_gather(w_back_loc, PLANE_AXES, axis=1, tiled=True)
            mixed = jnp.concatenate([attn.reshape(num_tokens, width_q), mlp_act], axis=1)
            part_sum = jnp.dot(mixed, w_back, preferred_element_type=jnp.float32)
            hidden = hidden + lax.psum_scatter(part_sum, "mp", scatter_dimension=1, tiled=True)
        return hidden

    col_spec = P(None, PLANE_AXES, "mp")
    kv_spec = P(None, PLANE_AXES, None)
    row_spec = P(None, "mp", PLANE_AXES)
    return jax.shard_map(
        device_body,
        mesh=mesh,
        in_specs=(P(TOKEN_AXES, "mp"), P(TOKEN_AXES), P(TOKEN_AXES), col_spec, kv_spec, kv_spec, col_spec, col_spec, row_spec, row_spec, P(None, "mp")),
        out_specs=P(TOKEN_AXES, "mp"),
        check_vma=False,
    )
```

profile of v0, /device:TPU:103, one launch (start us, length us, event | category | flops | bytes accessed | tf_op | source)
XLA Modules:
  0.0 1253.8 jit_solution(18427615086403199035)
XLA Ops:
  6.6 2.7 bitcast_dynamic-update-slice_fusion.4
  9.2 1.8 bitcast_dynamic-update-slice_fusion.7
  11.0 1.8 bitcast_dynamic-update-slice_fusion.6
  12.8 8.6 bitcast_dynamic-update-slice_fusion.1
  21.5 4.7 bitcast_dynamic-update-slice_fusion
  26.3 1.3 copy-done.2
  27.7 6.9 slice_bitcast_fusion.1
  34.6 2.9 pad_maximum_fusion
  39.6 10.4 psum.14
  50.2 10.9 all_gather.18
  61.2 337.0 %all-gather.5.cloned.1.call-done = bf16[3072,13824]{1,0:T(8,128)(2,1)} async-done(((bf16[384,13824]{1,0:T(8,128)(2,1)}), bf16[3072,13824]{1,0:T(8,128)(2,1)}) %all-gather.5.cloned.1.call-update) | async-done | bytes 84934672 | tf_op jit(solution)/shard_map/all_gather | solution.py:56
  398.1 29.6 %convolution_convert_fusion.1 = bf16[64,13824]{1,0:T(8,128)(2,1)S(1)} fusion(bf16[64,3072]{1,0:T(8,128)(2,1)S(1)} %all_gather.18, bf16[3072,13824]{1,0:T(8,128)(2,1)} %all-gather.5.cloned.1.call-done), kind=kOutput, calls=%fused_computation.3 | convolution fusion | flops 5436702720 | bytes 87097344 | tf_op jit(solution)/shard_map/dot_general | solution.py:57
  429.7 167.9 %all-gather.7.cloned.1.call-done = bf16[7168,3072]{1,0:T(8,128)(2,1)} async-done(((bf16[7168,384]{1,0:T(8,128)(2,1)}), bf16[7168,3072]{1,0:T(8,128)(2,1)}) %all-gather.7.cloned.1.call-update) | async-done | bytes 44040208 | tf_op jit(solution)/shard_map/all_gather | solution.py:63
  597.7 18.3 %fusion.22 = f32[64,3072]{1,0:T(8,128)} fusion(bf16[7168,3072]{1,0:T(8,128)(2,1)} %all-gather.7.cloned.1.call-done, bf16[64,6144]{1,0:T(8,128)(2,1)S(1)} %fusion.11, bf16[64,1024]{1,0:T(8,128)(2,1)} %bitcast.95), kind=kOutput, calls=%fused_computation.40 | convolution fusion | flops 2820407296 | bytes 45744128 | tf_op jit(solution)/shard_map/dot_general | solution.py:65
  616.8 5.3 pad_maximum_fusion.1
  622.3 13.2 %reduce-scatter.3.cloned.1.call-done = f32[64,768]{1,0:T(8,128)} async-done(((f32[64,3072]{1,0:T(8,128)}), f32[64,768]{1,0:T(8,128)}) %reduce-scatter.3.cloned.1.call-update) | async-done | bytes 196624 | tf_op jit(solution)/shard_map/reduce_scatter | solution.py:66
  636.5 6.6 psum.15
  644.1 10.5 all_gather.21
  654.6 353.4 %all-gather.9.cloned.1.call-done = bf16[3072,13824]{1,0:T(8,128)(2,1)} async-done(((bf16[384,13824]{1,0:T(8,128)(2,1)}), bf16[3072,13824]{1,0:T(8,128)(2,1)}) %all-gather.9.cloned.1.call-update) | async-done | bytes 84934672 | tf_op jit(solution)/shard_map/all_gather | solution.py:56
  1008.0 29.6 %convolution_convert_fusion = bf16[64,13824]{1,0:T(8,128)(2,1)S(1)} fusion(bf16[64,3072]{1,0:T(8,128)(2,1)S(1)} %all_gather.21, bf16[3072,13824]{1,0:T(8,128)(2,1)} %all-gather.9.cloned.1.call-done), kind=kOutput, calls=%fused_computation.2 | convolution fusion | flops 5436702720 | bytes 87097344 | tf_op jit(solution)/shard_map/dot_general | solution.py:57
  1039.0 168.4 %all-gather.11.cloned.1.call-done = bf16[7168,3072]{1,0:T(8,128)(2,1)} async-done(((bf16[7168,384]{1,0:T(8,128)(2,1)}), bf16[7168,3072]{1,0:T(8,128)(2,1)}) %all-gather.11.cloned.1.call-update) | async-done | bytes 44040208 | tf_op jit(solution)/shard_map/all_gather | solution.py:63
  1207.4 18.4 %fusion.26 = f32[64,3072]{1,0:T(8,128)} fusion(bf16[7168,3072]{1,0:T(8,128)(2,1)} %all-gather.11.cloned.1.call-done, bf16[64,6144]{1,0:T(8,128)(2,1)S(1)} %fusion.10, bf16[64,1024]{1,0:T(8,128)(2,1)S(1)} %bitcast.96), kind=kOutput, calls=%fused_computation.44 | convolution fusion | flops 2820407296 | bytes 45744128 | tf_op jit(solution)/shard_map/dot_general | solution.py:65
  1225.9 19.4 %reduce-scatter.5.cloned.1.call-done = f32[64,768]{1,0:T(8,128)} async-done(((f32[64,3072]{1,0:T(8,128)}), f32[64,768]{1,0:T(8,128)}) %reduce-scatter.5.cloned.1.call-update) | async-done | bytes 196624 | tf_op jit(solution)/shard_map/reduce_scatter | solution.py:66
  1245.3 1.6 fusion.47
  (62 shorter events, 8.2 us)
Async XLA Ops:
  6.5 391.6 %all-gather.5.cloned.1.call-start = ((), (), s32[]{:S(2)}) async-start(), calls=%async_computation.2 | async-start | bytes 95551488 | tf_op jit(solution)/shard_map/all_gather | solution.py:56
  12.8 8.6 slice-start
  12.8 8.6 slice-start.1
  12.8 8.6 slice-start.2
  26.1 1.4 copy-start.2
  26.2 571.5 %all-gather.7.cloned.1.call-start = ((), (), s32[]{:S(2)}) async-start(), calls=%async_computation.3 | async-start | bytes 49545216 | tf_op jit(solution)/shard_map/all_gather | solution.py:63
  37.5 0.7 copy-start.6
  37.5 1.9 copy-start.4
  37.5 1.9 copy-start
  37.5 12.4 copy-start.3
  37.5 23.5 %copy-start.5 = (s32[64]{0:T(128)S(1)}, s32[64]{0:T(128)}, u32[]{:S(2)}) copy-start(s32[64]{0:T(128)} %param.12) | copy-start | bytes 772
  37.6 597.8 %reduce-scatter.3.cloned.1.call-start = ((), (), s32[]{:S(2)}) async-start(), calls=%async_computation.4 | async-start | bytes 983040 | tf_op jit(solution)/shard_map/reduce_scatter | solution.py:66
  616.1 391.9 %all-gather.9.cloned.1.call-start = ((), (), s32[]{:S(2)}) async-start(), calls=%async_computation.5 | async-start | bytes 95551488 | tf_op jit(solution)/shard_map/all_gather | solution.py:56
  616.7 590.7 %all-gather.11.cloned.1.call-start = ((), (), s32[]{:S(2)}) async-start(), calls=%async_computation.6 | async-start | bytes 49545216 | tf_op jit(solution)/shard_map/all_gather | solution.py:63
  622.2 623.1 %reduce-scatter.5.cloned.1.call-start = ((), (), s32[]{:S(2)}) async-start(), calls=%async_computation.7 | async-start | bytes 983040 | tf_op jit(solution)/shard_map/reduce_scatter | solution.py:66
  1207.4 37.9 %copy-start.1 = (f32[64,768]{1,0:T(8,128)S(1)}, f32[64,768]{1,0:T(8,128)}, u32[]{:S(2)}) copy-start(f32[64,768]{1,0:T(8,128)} %reduce-scatter.3.cloned.1.call-done) | copy-start | bytes 589828
Sparse Core Ops, SparseCore 0:
  26.3 371.7 all-gather.4
  399.7 197.8 all-gather.6
  616.2 19.2 reduce-scatter.2
  636.9 371.0 all-gather.8
  1009.5 197.8 all-gather.10
  1226.0 19.2 reduce-scatter.4
where the time goes:
time: 1260 us; the launch traced here: 1250 us
  waiting for transfers between devices  1060 us (84%)
  matrix products  96.9 us (8%)
  blocking collectives  38.3 us (3%)
  local copies, waits for them, and re-layouts  30 us (2%)
  between operations  14.4 us (1%)
  other arithmetic  13.8 us (1%)
    all_gather x2, waiting for transfers between devices, device_body(): w_in = lax.all_gather(w_in_loc, PLANE_AXES, axis=0, tiled=True)  690 us
    all_gather x2, waiting for transfers between devices, device_body(): w_back = lax.all_gather(w_back_loc, PLANE_AXES, axis=1, tiled=True)  336 us
    dot_general x2, matrix products, device_body(): jnp.dot(normed, w_in, preferred_element_type=jnp.float32)  59.1 us
    dot_general x2, matrix products, device_body(): part_sum = jnp.dot(mixed, w_back, preferred_element_type=jnp.float32)  36.8 us
    reduce_scatter x2, waiting for transfers between devices, device_body(): lax.psum_scatter(part_sum, 'mp', scatter_dimension=1, tiled=True)  32.6 us
  transfers between devices with their start and end apart: 6, of which 6 were waited for; matrix products, arithmetic and copies ran while one was open for 6% of the time, Pallas kernels for 0%

commit v1 on v0

v1 whole, which is shorter than its diff:
```python
import functools

import jax
import jax.numpy as jnp
from jax import lax
from jax.experimental import pallas as pl
from jax.experimental.pallas import tpu as pltpu
from jax.sharding import PartitionSpec as P

ROPE_BASE = 10000.0
NORM_EPS = 1e-6
TOKEN_AXES = ("rep", "tb", "ta")
PLANE_AXES = ("tb", "ta")
MESH = pl.DeviceIdType.MESH
BF16, F32 = jnp.bfloat16, jnp.float32
NX, NY = 4, 4
CW = 256


def al(index, unit):
    return pl.multiple_of(index, unit)


def kernel(dims, x_ref, pack_ref, freq_ref, gain_ref, wq, wkv, wg, wu, wo, wd, out_ref,
           w_at, w_ml, wb, zs, zr, za, zar, m_buf, h_buf, acc, res, kv_buf, q_buf, cos_t, sin_t, packs,
           stat_own, stat_in, rs_in, x_in, f_in,
           xs_s, xs_r, ps_s, ps_r, w_s, wa_s, w_r, wa_r, wb_r, p_s, p_r, ring_s, ring_r, d_s, d_r,
           kv_s, kv_r, h_s, h_r, y_s, y_r, st_s, st_r, rs_s, rs_r, f_s, f_r):
    layers, blk, kw, gq, gkv, gff = dims
    nch = gff // CW
    tok = 8 * blk
    half = tok // 2
    tb2 = 2 * blk
    x, c, y = lax.axis_index("tb"), lax.axis_index("ta"), lax.axis_index("mp")
    right, left = (x + 1) % NX, (x + NX - 1) % NX
    nxt = right * (1 - c) + left * c
    group = (x + NX - c) % NX

    def dev(tb=None, ta=None, mp=None):
        return {"tb": x if tb is None else tb, "ta": c if ta is None else ta, "mp": y if mp is None else mp}

    sib = dev(ta=1 - c)
    ring = dev(tb=nxt)
    partner = dev(tb=nxt, ta=1 - c)

    def send(src, dst, ssem, rsem, to):
        pltpu.make_async_remote_copy(src_ref=src, dst_ref=dst, send_sem=ssem, recv_sem=rsem, device_id=to, device_id_type=MESH).start()

    def local(src, dst, sem):
        pltpu.make_async_copy(src, dst, sem).start()

    def wait(ref, sem):
        pltpu.make_async_copy(ref, ref, sem).wait()

    me_plane = 2 * x + c
    barrier = pltpu.get_barrier_semaphore()
    for d in range(1, 2 * NX):
        q = (me_plane + d) % (2 * NX)
        pl.semaphore_signal(barrier, inc=1, device_id=dev(tb=q // 2, ta=q % 2), device_id_type=MESH)
    for d in range(1, NY):
        pl.semaphore_signal(barrier, inc=1, device_id=dev(mp=(y + d) % NY), device_id_type=MESH)

    peers = 2 * NX - 1 + NY - 1

    @pl.when(x != y)
    def _():
        for t in range(2):
            pl.semaphore_signal(barrier, inc=1, device_id=dev(tb=y, ta=t, mp=x), device_id_type=MESH)
        pl.semaphore_wait(barrier, peers + 2)

    @pl.when(x == y)
    def _():
        pl.semaphore_wait(barrier, peers)

    def swap_start(src_of, dst, ssem, rsem):
        for t in range(2):
            own = jnp.logical_and(x == y, c == t)

            @pl.when(own)
            def _():
                local(src_of(t), dst, rsem.at[c])

            @pl.when(jnp.logical_not(own))
            def _():
                send(src_of(t), dst, ssem.at[t], rsem.at[c], dev(tb=y, ta=t, mp=x))

    def swap_wait(part, ssem, rsem):
        for t in range(2):
            wait(part, rsem.at[t])

            @pl.when(jnp.logical_not(jnp.logical_and(x == y, c == t)))
            def _():
                wait(part, ssem.at[t])

    swap_start(lambda t: x_ref.at[:, t * kw:(t + 1) * kw], x_in.at[pl.ds(al(c * blk, blk), blk)], xs_s, xs_r)

    pack_slot = (x % 2) * 2 + c
    pack_core = x // 2
    pack_own = c == pack_core

    @pl.when(pack_own)
    def _():
        local(pack_ref, packs.at[pack_slot], ps_r)

    @pl.when(jnp.logical_not(pack_own))
    def _():
        send(pack_ref, packs.at[pack_slot], ps_s.at[0], ps_r, dev(ta=pack_core))

    for d in range(1, NX):
        send(pack_ref, packs.at[pack_slot], ps_s.at[d], ps_r, dev(tb=(x + d) % NX, ta=pack_core))

    def issue_w(layer, idx):
        targets = (
            ((x + 1) % NX, c, dev(tb=right, ta=0)),
            ((x + 2) % NX, c, dev(tb=left, ta=1)),
            ((x + 3 + c) % NX, 2 + c, sib),
            (group, 2 + c, None),
        )
        for grp, slot, to in targets:
            rows = pl.ds(al(slot * kw, kw), kw)
            if idx == 0:
                pieces = (
                    (wq.at[layer, :, pl.ds(al(grp * gq, gq), gq)], w_at.at[layer, rows, 0:gq]),
                    (wkv.at[layer, :, pl.ds(al(grp * gkv, gkv), gkv)], w_at.at[layer, rows, gq:gq + gkv]),
                )
                ssem, rsem = wa_s.at[layer], wa_r.at[layer]
            else:
                j = idx - 1
                cols = pl.ds(al(grp * gff + j * CW, CW), CW)
                pieces = (
                    (wg.at[layer, :, cols], w_ml.at[layer, j, rows, 0:CW]),
                    (wu.at[layer, :, cols], w_ml.at[layer, j, rows, CW:2 * CW]),
                )
                ssem, rsem = w_s.at[layer], w_r.at[layer, j]
            for src, dst in pieces:
                if to is None:
                    local(src, dst, rsem)
                else:
                    send(src, dst, ssem, rsem, to)

    for idx in range(3):
        issue_w(0, idx)

    swap_wait(x_in.at[0:blk], xs_s, xs_r)
    res[...] = x_in[...].astype(F32)

    wait(packs, ps_r)
    for b in range(4):
        ang = packs[b, :, 128:256].astype(F32) * freq_ref[0:1, :]
        cos_t[b * blk:(b + 1) * blk, :] = jnp.cos(ang)
        sin_t[b * blk:(b + 1) * blk, :] = jnp.sin(ang)

    def rope(v, rows):
        lo, hi = v[:, 0:128].astype(F32), v[:, 128:256].astype(F32)
        cs, sn = cos_t[rows, :], sin_t[rows, :]
        return jnp.concatenate([lo * cs - hi * sn, hi * cs + lo * sn], axis=1).astype(BF16)

    own_rows = pl.ds(al(c * half, half), half)
    far_rows = pl.ds(al((1 - c) * half, half), half)
    y_rows = pl.ds(al(y * tb2, tb2), tb2)

    def group_at(s):
        return ((x + NX - s) * (1 - c) + (x + s - 1) * c) % NX

    def layer_body(layer, carry):
        for g in range(NX):
            for j in range(nch):
                local(wd.at[layer, g * gff + j * CW:g * gff + (j + 1) * CW], wb.at[j, g * CW:(g + 1) * CW], wb_r.at[layer])
        local(wo.at[layer], wb.at[nch], wb_r.at[layer])

        r = res[...]
        ssum = jnp.sum(r * r, axis=1, keepdims=True)
        stat = jnp.broadcast_to(ssum, (tb2, 128)).T[0:8]
        stat_own[...] = stat
        for d in range(1, 2 * NX):
            q = (me_plane + d) % (2 * NX)
            send(stat_own, stat_in.at[layer, d - 1], st_s.at[layer], st_r.at[layer], dev(tb=q // 2, ta=q % 2))
        issue_w(layer, 3)
        wait(stat_in.at[layer], st_r.at[layer])
        total = stat
        for d in range(2 * NX - 1):
            total = total + stat_in[layer, d]
        mean = jnp.broadcast_to(total[0:1], (128, tb2)).T[:, 0:1] / (kw * 2 * NX)
        normed = (r * lax.rsqrt(mean + NORM_EPS) * gain_ref[layer]).astype(BF16)
        own_cols = pl.ds(al((2 + c) * kw, kw), kw)
        h_buf[y_rows, own_cols] = normed
        mine = h_buf.at[y_rows, own_cols]
        send(mine, h_buf.at[y_rows, pl.ds(al(c * kw, kw), kw)], h_s.at[layer], h_r.at[layer], dev(tb=right, ta=0))
        send(mine, h_buf.at[y_rows, pl.ds(al(c * kw, kw), kw)], h_s.at[layer], h_r.at[layer], dev(tb=left, ta=1))
        send(mine, mine, h_s.at[layer], h_r.at[layer], sib)
        for d in range(1, NY):
            send(mine, mine, y_s.at[layer], y_r.at[layer], dev(mp=(y + d) % NY))
        issue_w(layer, 4)
        wait(h_buf.at[0:3 * tb2, 0:kw], h_r.at[layer])
        near = h_buf.at[y_rows, 0:2 * kw]
        other = h_buf.at[y_rows, pl.ds(al((3 - c) * kw, kw), kw)]
        for d in range(1, NY):
            send(near, near, y_s.at[layer], y_r.at[layer], dev(mp=(y + d) % NY))
        for d in range(1, NY):
            send(other, other, y_s.at[layer], y_r.at[layer], dev(mp=(y + d) % NY))
        acc[...] = jnp.zeros_like(acc)
        wait(h_buf.at[0:3 * tb2, :], y_r.at[layer])

        def share(j, g):
            blkref = m_buf.at[j, c, g]
            send(blkref, blkref, d_s.at[layer], d_r.at[layer, j], sib)

        def stage_m_out(j, m):
            m_buf[j, c, group] = m
            blkref = m_buf.at[j, c, group]
            send(blkref, blkref, ring_s.at[layer], ring_r.at[layer, j, 0], ring)
            share(j, group)

        def stage_r(j, s):
            g = group_at(s)
            blkref = m_buf.at[j, c, g]
            wait(blkref, ring_r.at[layer, j, s - 1])
            if s < NX - 1:
                send(blkref, blkref, ring_s.at[layer], ring_r.at[layer, j, s], ring)
            share(j, g)

        def stage_d(j):
            wait(m_buf.at[j, 1 - c], d_r.at[layer, j])
            for hf in range(2):
                lhs = jnp.concatenate([m_buf[j, hf, g] for g in range(NX)], axis=1)
                acc[hf * half:(hf + 1) * half, :] += jnp.dot(lhs, wb[j], preferred_element_type=F32)

        def stage_p(j):
            wait(w_ml.at[layer, j], w_r.at[layer, j])
            for n in range(2):
                zs[j, :, n * CW:(n + 1) * CW] = jnp.dot(h_buf[...], w_ml[layer, j, :, n * CW:(n + 1) * CW], preferred_element_type=F32)
            send(zs.at[j, far_rows], zr.at[j], p_s.at[layer, j], p_r.at[layer, j], partner)

        def stage_m(j):
            wait(zr.at[j], p_r.at[layer, j])
            z = zs[j, own_rows, :] + zr[j]
            gate = z[:, 0:CW].astype(BF16).astype(F32)
            up = z[:, CW:2 * CW].astype(BF16).astype(F32)
            stage_m_out(j, (jax.nn.silu(gate) * up).astype(BF16))

        def attn_p():
            wait(w_at.at[layer], wa_r.at[layer])
            za[...] = jnp.dot(h_buf[...], w_at[layer], preferred_element_type=F32)
            send(za.at[far_rows], zar, p_s.at[layer, nch], p_r.at[layer, nch], partner)

        def attn_m():
            wait(zar, p_r.at[layer, nch])
            z = za[own_rows, :] + zar[...]
            q_buf[...] = z[:, 0:gq].astype(BF16)
            kv_buf[group] = z[:, gq:gq + gkv].astype(BF16)
            send(kv_buf.at[group], kv_buf.at[group], kv_s.at[layer], kv_r.at[layer, 0], ring)

        def attn_r(s):
            g = group_at(s)
            wait(kv_buf.at[g], kv_r.at[layer, s - 1])
            if s < NX - 1:
                send(kv_buf.at[g], kv_buf.at[g], kv_s.at[layer], kv_r.at[layer, s], ring)

        def attn_core():
            outs = []
            for b in range(4):
                rows = slice(b * blk, (b + 1) * blk)
                q = rope(q_buf[rows, :], rows)
                k = rope(jnp.concatenate([kv_buf[0, rows, :], kv_buf[1, rows, :]], axis=1), rows)
                v = jnp.concatenate([kv_buf[2, rows, :], kv_buf[3, rows, :]], axis=1)
                scores = lax.dot_general(q, k, (((1,), (1,)), ((), ())), preferred_element_type=F32) * (gq ** -0.5)
                scores = jnp.where(packs[b, :, 0:blk].astype(F32) > 0.5, scores, -1e30)
                ex = jnp.exp(scores - jnp.max(scores, axis=1, keepdims=True))
                prob = (ex / jnp.sum(ex, axis=1, keepdims=True)).astype(BF16)
                outs.append(jnp.dot(prob, v, preferred_element_type=F32).astype(BF16))
            stage_m_out(nch, jnp.concatenate(outs, axis=0))

        for t in range(nch + 5):
            if 0 <= t - 4 < nch:
                stage_r(t - 4, 3)
            if t == 7:
                stage_r(nch, 3)
            if 0 <= t - 3 < nch:
                stage_r(t - 3, 2)
            if t == 6:
                stage_r(nch, 2)
            if 0 <= t - 2 < nch:
                stage_r(t - 2, 1)
            if t == 5:
                stage_r(nch, 1)
            if t == 0:
                attn_p()
            if t in (2, 3, 4):
                attn_r(t - 1)
            if 0 <= t - 1 < nch:
                stage_m(t - 1)
            if t == 1:
                attn_m()
            if t < nch:
                stage_p(t)
            if t in (0, 1):
                issue_w(layer, 5 + t)
            if t in (7, 8, 9):
                @pl.when(layer < layers - 1)
                def _():
                    issue_w(layer + 1, t - 7)
            if t == 4:
                attn_core()
            if t == 5:
                wait(wb, wb_r.at[layer])
            if 0 <= t - 5 < nch:
                stage_d(t - 5)
            if t == 8:
                stage_d(nch)

        for d in range(1, NY):
            to = (y + d) % NY
            send(acc.at[pl.ds(al(to * tb2, tb2), tb2)], rs_in.at[d - 1], rs_s.at[layer], rs_r.at[layer], dev(mp=to))
        wait(rs_in, rs_r.at[layer])
        res[...] = res[...] + (acc[y_rows, :] + rs_in[0] + rs_in[1] + rs_in[2])

        wait(stat_in.at[layer], st_s.at[layer])
        wait(h_buf.at[0:3 * tb2, 0:kw], h_s.at[layer])
        wait(h_buf.at[0:3 * tb2, :], y_s.at[layer])
        for j in range(nch):
            wait(zr.at[j], p_s.at[layer, j])
        wait(zar, p_s.at[layer, nch])
        wait(kv_buf.at[0:NX - 1], kv_s.at[layer])
        wait(m_buf.at[:, 0, 0:NX - 1], ring_s.at[layer])
        wait(m_buf.at[:, 0], d_s.at[layer])
        wait(rs_in, rs_s.at[layer])
        wait(w_at.at[layer, 0:3 * kw], wa_s.at[layer])
        wait(w_ml.at[layer, :, 0:3 * kw], w_s.at[layer])
        return carry

    lax.fori_loop(0, layers, layer_body, 0)

    swap_start(lambda t: res.at[t * blk:(t + 1) * blk], f_in.at[:, pl.ds(al(c * kw, kw), kw)], f_s, f_r)
    swap_wait(res.at[0:blk], f_s, f_r)
    out_ref[...] = f_in[...]

    @pl.when(jnp.logical_not(pack_own))
    def _():
        wait(pack_ref, ps_s.at[0])

    for d in range(1, NX):
        wait(pack_ref, ps_s.at[d])


def solution(mesh):
    def device_body(x_loc, seg_ids, pos_ids, w_q, w_k, w_v, w_gate, w_up, w_out, w_down, gain):
        blk, width_loc = x_loc.shape
        layers, kw, _ = w_q.shape
        head_dim = w_k.shape[-1]
        gq = w_q.shape[-1] // NX
        gff = w_gate.shape[-1] // NX
        gkv = 2 * head_dim // NX
        nch = gff // CW
        tok, half, tb2 = 8 * blk, 4 * blk, 2 * blk
        kg = 4 * kw
        allowed = (seg_ids[:, None] == seg_ids[None, :]) & (pos_ids[None, :] <= pos_ids[:, None])
        pack = jnp.concatenate([
            jnp.pad(allowed.astype(BF16), ((0, 0), (0, 128 - blk))),
            jnp.broadcast_to(pos_ids.astype(BF16)[:, None], (blk, 128)),
        ], axis=1)
        half_dim = head_dim // 2
        freq = ROPE_BASE ** (-(jnp.arange(half_dim, dtype=F32) * 2.0) / head_dim)
        freq = jnp.broadcast_to(freq[None], (8, half_dim))
        place = 2 * lax.axis_index("tb") + lax.axis_index("ta")
        gain_loc = lax.dynamic_slice(gain, (0, place * kw), (layers, kw)).astype(F32)[:, None, :]
        wkv = jnp.concatenate([w_k, w_v], axis=-1)
        hbm = pl.BlockSpec(memory_space=pl.ANY)
        vmem = pl.BlockSpec(memory_space=pltpu.VMEM)
        dma = pltpu.SemaphoreType.DMA
        return pl.pallas_call(
            functools.partial(kernel, (layers, blk, kw, gq, gkv, gff)),
            out_shape=jax.ShapeDtypeStruct((blk, width_loc), F32),
            in_specs=[vmem] * 4 + [hbm] * 6,
            out_specs=vmem,
            scratch_shapes=[
                pltpu.VMEM((layers, kg, gq + gkv), BF16),
                pltpu.VMEM((layers, nch, kg, 2 * CW), BF16),
                pltpu.VMEM((nch + 1, NX * CW, kw), BF16),
                pltpu.VMEM((nch, tok, 2 * CW), F32),
                pltpu.VMEM((nch, half, 2 * CW), F32),
                pltpu.VMEM((tok, gq + gkv), F32),
                pltpu.VMEM((half, gq + gkv), F32),
                pltpu.VMEM((nch + 1, 2, NX, half, CW), BF16),
                pltpu.VMEM((tok, kg), BF16),
                pltpu.VMEM((tok, kw), F32),
                pltpu.VMEM((tb2, kw), F32),
                pltpu.VMEM((NX, half, gkv), BF16),
                pltpu.VMEM((half, gq), BF16),
                pltpu.VMEM((half, half_dim), F32),
                pltpu.VMEM((half, half_dim), F32),
                pltpu.VMEM((4, blk, 256), BF16),
                pltpu.VMEM((8, tb2), F32),
                pltpu.VMEM((layers, 2 * NX - 1, 8, tb2), F32),
                pltpu.VMEM((NY - 1, tb2, kw), F32),
                pltpu.VMEM((tb2, kw), BF16),
                pltpu.VMEM((blk, width_loc), F32),
                dma((2,)), dma((2,)), dma((NX,)), dma(()),
                dma((layers,)), dma((layers,)), dma((layers, nch)), dma((layers,)), dma((layers,)),
                dma((layers, nch + 1)), dma((layers, nch + 1)),
                dma((layers,)), dma((layers, nch + 1, NX - 1)), dma((layers,)), dma((layers, nch + 1)),
                dma((layers,)), dma((layers, NX - 1)), dma((layers,)), dma((layers,)),
                dma((layers,)), dma((layers,)), dma((layers,)), dma((layers,)), dma((layers,)), dma((layers,)),
                dma((2,)), dma((2,)),
            ],
            compiler_params=pltpu.CompilerParams(collective_id=0, has_side_effects=True, vmem_limit_bytes=60 * 1024 * 1024),
        )(x_loc, pack, freq, gain_loc, w_q, wkv, w_gate, w_up, w_out, w_down)

    col_spec = P(None, PLANE_AXES, "mp")
    kv_spec = P(None, PLANE_AXES, None)
    row_spec = P(None, "mp", PLANE_AXES)
    return jax.shard_map(
        device_body,
        mesh=mesh,
        in_specs=(P(TOKEN_AXES, "mp"), P(TOKEN_AXES), P(TOKEN_AXES), col_spec, kv_spec, kv_spec, col_spec, col_spec, row_spec, row_spec, P(None, None)),
        out_specs=P(TOKEN_AXES, "mp"),
        check_vma=False,
    )
```

time: 1260 us -> 331 us (0.26)
  waiting for transfers between devices: 1060 us -> 0 us
  Pallas kernels: 0 us -> 322 us
  matrix products: 96.9 us -> 0 us
  blocking collectives: 38.3 us -> 0 us
  local copies, waits for them, and re-layouts: 30 us -> 2.87 us
  between operations: 14.4 us -> 0.03 us
    all_gather x4 -> x0, waiting for transfers between devices: 1030 us -> none  [the longest x2 690 us: device_body(): w_in = lax.all_gather(w_in_loc, PLANE_AXES, axis=0, tiled=True)]
    pallas_call x0 -> x1, Pallas kernels: none -> 322 us  [device_body(): pl.pallas_call(functools.partial(kernel, (layers, blk, kw, gq, gkv, gff))...]
    dot_general x6 -> x0, matrix products: 96.4 us -> none  [the longest x2 59.1 us: device_body(): jnp.dot(normed, w_in, preferred_element_type=jnp.float32)]
    reduce_scatter x2 -> x0, waiting for transfers between devices: 32.6 us -> none  [device_body(): lax.psum_scatter(part_sum, 'mp', scatter_dimension=1, tiled=True)]
    all_gather x2 -> x0, blocking collectives: 21.4 us -> none  [device_body(): normed = lax.all_gather(normed_loc, 'mp', axis=1, tiled=True)]
    psum x2 -> x0, blocking collectives: 17 us -> none  [device_body(): mean_sq = lax.psum(sq_part, 'mp') / (embed_loc * mp_size)]
    unnamed x24 -> x1, local copies, waits for them, and re-layouts: 16.7 us -> 1.62 us
  transfers between devices with their start and end apart: 6 -> 0, of which waited for: 6 -> 0; matrix products, arithmetic and copies ran while one was open for 6% -> 0% of each run, Pallas kernels for 0% -> 0%
where the time goes in v1:
time: 331 us; the launch traced here: 330 us
  Pallas kernels  322 us (97%)
  other arithmetic  4.85 us (1%)
    pallas_call x1, Pallas kernels, device_body(): pl.pallas_call(functools.partial(kernel, (layers, blk, kw, gq, gkv, gff))...  322 us

profile of v1, /device:TPU:103, one launch (start us, length us, event | category | flops | bytes accessed | tf_op | source)
XLA Modules:
  0.0 330.1 jit_solution(6806496521291920101)
XLA Ops:
  0.0 0.7 convert_element_type.4
  0.7 0.7 dynamic-slice_convert_fusion
  1.4 0.6 reshape.12.gain_ref
  2.0 0.6 broadcast_in_dim.9.freq_ref
  2.5 0.8 compare_and_fusion
  3.4 0.1 broadcast_in_dim.8
  3.5 0.6 pad_maximum_fusion.1.pack_ref
  4.1 2.0 pad_maximum_fusion.wkv
  6.1 322.3 %shard_map.109 = f32[64,768]{1,0:T(8,128)} custom-call(bf16[64,768]{1,0:T(8,128)(2,1)} %x_ref.1, bf16[64,256]{1,0:T(8,128)(2,1)} %pad_maximum_fusion.1.pack_ref, f32[8,128]{1,0:T(8,128)} %broadcast_in_dim.9.freq_ref, f32[2,1,384]{2,1,0:T(1,128)} %reshape.12.gain_ref, bf16[2,384,1024]{2,1,0:T(8,128)(2,1)} %wq.1, bf16[2,384,512]{2,1,0:T(8,128)(2,1)} %pad_maximum_fusion.wkv, ...), custom_call_target="tpu_custom_call" | custom-call | tf_op jit(solution)/shard_map/pallas_call | solution.py:370
  328.5 1.6 copy.13
  (2 shorter events, 0.0 us)

commit v2 on v1

v2 whole, which is shorter than its diff:
```python
import functools
import math

import jax
import jax.numpy as jnp
from jax import lax
from jax.experimental import pallas as pl
from jax.experimental.pallas import tpu as pltpu
from jax.sharding import PartitionSpec as P

ROPE_BASE = 10000.0
NORM_EPS = 1e-6
TOKEN_AXES = ("rep", "tb", "ta")
PLANE_AXES = ("tb", "ta")
MESH = pl.DeviceIdType.MESH
BF16, F32 = jnp.bfloat16, jnp.float32
NX, NY = 4, 4
CW = 256


def al(index, unit):
    return pl.multiple_of(index, unit)


def kernel(dims, x_ref, seg_ref, pos_ref, gain_ref, wq, wk, wv, wg, wu, wo, wd, out_ref,
           w_at, w_ml, wb, zs, zr, za, zar, zkv, m_buf, h_buf, acc, res, kv_buf, q_buf, cos_t, sin_t, packs,
           stat_own, stat_in, rs_in, rl_in, x_in, f_in, pack_ref, ids_t,
           xs_s, xs_r, ps_s, ps_r, w_s, wa_s, w_r, wa_r, wb_r, p_s, p_r, ring_s, ring_r, d_s, d_r,
           kv_s, kv_r, h_s, h_r, y_s, y_r, y0_s, y0_r, sb_s, sb_r, st_s, st_r, rs_s, rs_r, rl_s, rl_r, f_s, f_r, kvx_s, kvx_r, kvy_s, kvy_r, kvp_s, kvp_r, kvz_s, kvz_r):
    layers, blk, kw, gq, gkv, gff = dims
    nch = gff // CW
    tok = 8 * blk
    half = tok // 2
    tb2 = 2 * blk
    x, c, y = lax.axis_index("tb"), lax.axis_index("ta"), lax.axis_index("mp")
    right, left = (x + 1) % NX, (x + NX - 1) % NX
    nxt = right * (1 - c) + left * c
    prv = left * (1 - c) + right * c
    group = (x + NX - c) % NX

    def dev(tb=None, ta=None, mp=None):
        return {"tb": x if tb is None else tb, "ta": c if ta is None else ta, "mp": y if mp is None else mp}

    sib = dev(ta=1 - c)
    ring = dev(tb=nxt)
    partner = dev(tb=nxt, ta=1 - c)

    def send(src, dst, ssem, rsem, to):
        pltpu.make_async_remote_copy(src_ref=src, dst_ref=dst, send_sem=ssem, recv_sem=rsem, device_id=to, device_id_type=MESH).start()

    def local(src, dst, sem):
        pltpu.make_async_copy(src, dst, sem).start()

    def wait(ref, sem):
        pltpu.make_async_copy(ref, ref, sem).wait()

    me_plane = 2 * x + c
    barrier = pltpu.get_barrier_semaphore()
    for d in range(1, 2 * NX):
        q = (me_plane + d) % (2 * NX)
        pl.semaphore_signal(barrier, inc=1, device_id=dev(tb=q // 2, ta=q % 2), device_id_type=MESH)
    for d in range(1, NY):
        pl.semaphore_signal(barrier, inc=1, device_id=dev(mp=(y + d) % NY), device_id_type=MESH)

    peers = 2 * NX - 1 + NY - 1

    @pl.when(x != y)
    def _():
        for t in range(2):
            pl.semaphore_signal(barrier, inc=1, device_id=dev(tb=y, ta=t, mp=x), device_id_type=MESH)
        pl.semaphore_wait(barrier, peers + 2)

    @pl.when(x == y)
    def _():
        pl.semaphore_wait(barrier, peers)

    def swap_start(src_of, dst, ssem, rsem):
        for t in range(2):
            own = jnp.logical_and(x == y, c == t)

            @pl.when(own)
            def _():
                local(src_of(t), dst, rsem.at[c])

            @pl.when(jnp.logical_not(own))
            def _():
                send(src_of(t), dst, ssem.at[t], rsem.at[c], dev(tb=y, ta=t, mp=x))

    def swap_wait(part, ssem, rsem):
        for t in range(2):
            wait(part, rsem.at[t])

            @pl.when(jnp.logical_not(jnp.logical_and(x == y, c == t)))
            def _():
                wait(part, ssem.at[t])

    swap_start(lambda t: x_ref.at[:, t * kw:(t + 1) * kw], x_in.at[pl.ds(al(c * blk, blk), blk)], xs_s, xs_r)

    qr = kw // NY

    def kv_quarter(slot):
        return pl.ds(al(slot * kw + y * qr, qr), qr)

    def kv_spread(layer):
        wait(w_at.at[layer, 0:2 * qr, gq:gq + gkv], kvx_r.at[layer])
        for d in range(1, NY):
            for slot in range(2):
                piece = w_at.at[layer, kv_quarter(slot), gq:gq + gkv]
                send(piece, piece, kvy_s.at[layer], kvy_r.at[layer], dev(mp=(y + d) % NY))

    def issue_w(layer, idx, part):
        if part == 0:
            targets = (((prv + NX + c - 1) % NX, c, dev(tb=prv, ta=1 - c)), ((x + 3 + c) % NX, 2 + c, sib), (group, 2 + c, None))
        else:
            targets = (((nxt + NX - c) % NX, c, ring),)
        for grp, slot, to in targets:
            rows = pl.ds(al(slot * kw, kw), kw)

            def put(src, dst, ssem, rsem):
                if to is None:
                    local(src, dst, rsem)
                else:
                    send(src, dst, ssem, rsem, to)

            if idx == 0:
                ssem, rsem = wa_s.at[layer], wa_r.at[layer]
                put(wq.at[layer, :, pl.ds(al(grp * gq, gq), gq)], w_at.at[layer, rows, 0:gq], ssem, rsem)
                kv_cols = pl.ds(al((grp % 2) * gkv, gkv), gkv)
                if to is None or to is sib:
                    kv_src, kv_rows, kv_sems = slice(None), rows, (ssem, rsem)
                else:
                    kv_src, kv_rows, kv_sems = pl.ds(al(y * qr, qr), qr), kv_quarter(slot), (kvx_s.at[layer], kvx_r.at[layer])
                kv_dst = w_at.at[layer, kv_rows, gq:gq + gkv]

                @pl.when(grp < 2)
                def _():
                    put(wk.at[layer, kv_src, kv_cols], kv_dst, *kv_sems)

                @pl.when(grp >= 2)
                def _():
                    put(wv.at[layer, kv_src, kv_cols], kv_dst, *kv_sems)
            else:
                j = idx - 1
                cols = pl.ds(al(grp * gff + j * CW, CW), CW)
                ssem, rsem = w_s.at[layer], w_r.at[layer, j]
                put(wg.at[layer, :, cols], w_ml.at[layer, j, rows, 0:CW], ssem, rsem)
                put(wu.at[layer, :, cols], w_ml.at[layer, j, rows, CW:2 * CW], ssem, rsem)

    issue_w(0, 0, 0)
    issue_w(0, 0, 1)

    ids_t[...] = jnp.zeros_like(ids_t)
    ids_t[:, 0:blk] = jnp.broadcast_to(seg_ref[...], (128, blk))
    seg_rows, seg_cols = ids_t[0:blk, 0:blk], ids_t[...].T[0:blk, 0:blk]
    ids_t[:, 0:blk] = jnp.broadcast_to(pos_ref[...], (128, blk))
    pos_rows, pos_cols = ids_t[0:blk, 0:blk], ids_t[...].T[0:blk]
    allowed = (seg_rows == seg_cols) & (pos_rows <= pos_cols[:, 0:blk])
    pack_ref[...] = jnp.zeros_like(pack_ref)
    pack_ref[:, 0:blk] = jnp.where(allowed, 1.0, 0.0).astype(BF16)
    pack_ref[:, 128:256] = pos_cols.astype(F32).astype(BF16)

    pack_slot = (x % 2) * 2 + c
    pack_core = x // 2
    pack_own = c == pack_core

    @pl.when(pack_own)
    def _():
        local(pack_ref, packs.at[pack_slot], ps_r)

    @pl.when(jnp.logical_not(pack_own))
    def _():
        send(pack_ref, packs.at[pack_slot], ps_s.at[0], ps_r, dev(ta=pack_core))

    for d in range(1, NX):
        send(pack_ref, packs.at[pack_slot], ps_s.at[d], ps_r, dev(tb=(x + d) % NX, ta=pack_core))

    for idx in (1, 2):
        issue_w(0, idx, 0)
        issue_w(0, idx, 1)
    swap_wait(x_in.at[0:blk], xs_s, xs_r)
    res[...] = x_in[...].astype(F32)

    def tables():
        wait(packs, ps_r)
        lane = lax.broadcasted_iota(jnp.int32, (8, gq // 2), 1).astype(F32)
        freq = jnp.exp(lane * (-2.0 * math.log(ROPE_BASE) / gq))[0:1]
        for b in range(4):
            ang = packs[b, :, 128:256].astype(F32) * freq
            cos_t[b * blk:(b + 1) * blk, :] = jnp.cos(ang)
            sin_t[b * blk:(b + 1) * blk, :] = jnp.sin(ang)

    def rope(v, rows):
        lo, hi = v[:, 0:128].astype(F32), v[:, 128:256].astype(F32)
        cs, sn = cos_t[rows, :], sin_t[rows, :]
        return jnp.concatenate([lo * cs - hi * sn, hi * cs + lo * sn], axis=1).astype(BF16)

    own_rows = pl.ds(al(c * half, half), half)
    far_rows = pl.ds(al((1 - c) * half, half), half)
    y_rows = pl.ds(al(y * tb2, tb2), tb2)

    def group_at(s):
        return ((x + NX - s) * (1 - c) + (x + s - 1) * c) % NX

    def issue_all(layer, units):
        for idx, part in units:
            issue_w(layer, idx, part)

    def layer_body(layer, carry):
        for g in range(NX):
            for j in range(nch):
                local(wd.at[layer, g * gff + j * CW:g * gff + (j + 1) * CW], wb.at[j, g * CW:(g + 1) * CW], wb_r.at[layer])
        local(wo.at[layer], wb.at[nch], wb_r.at[layer])

        r = res[...]
        ssum = jnp.sum(r * r, axis=1, keepdims=True)
        stat = jnp.broadcast_to(ssum, (tb2, 128)).T[0:8]
        stat_own[...] = stat
        for d in range(1, 2 * NX):
            q = (me_plane + d) % (2 * NX)
            send(stat_own, stat_in.at[layer, d - 1], st_s.at[layer], st_r.at[layer], dev(tb=q // 2, ta=q % 2))
        issue_all(layer, ((3, 0), (3, 1)))
        wait(stat_in.at[layer], st_r.at[layer])
        total = stat
        for d in range(2 * NX - 1):
            total = total + stat_in[layer, d]
        mean = jnp.broadcast_to(total[0:1], (128, tb2)).T[:, 0:1] / (kw * 2 * NX)
        gains = gain_ref[:, pl.ds(al(me_plane * kw, 128), kw)].astype(F32)
        gain = jnp.where(layer == 0, gains[0:1], gains[1:2])
        normed = (r * lax.rsqrt(mean + NORM_EPS) * gain).astype(BF16)
        own_cols = pl.ds(al((2 + c) * kw, kw), kw)
        h_buf[y_rows, own_cols] = normed
        mine = h_buf.at[y_rows, own_cols]
        far = h_buf.at[y_rows, pl.ds(al(c * kw, kw), kw)]
        send(mine, far, h_s.at[layer], h_r.at[layer], dev(tb=right, ta=0))
        send(mine, far, h_s.at[layer], h_r.at[layer], dev(tb=left, ta=1))
        for d in range(1, NY):
            send(mine, mine, y0_s.at[layer], y0_r.at[layer], dev(mp=(y + d) % NY))
        issue_all(layer, ((4, 0), (4, 1), (5, 0)))
        acc[...] = jnp.zeros_like(acc)
        wait(h_buf.at[y_rows, 0:2 * kw], h_r.at[layer])
        near = h_buf.at[y_rows, 0:2 * kw]
        for d in range(1, NY):
            send(near, near, y_s.at[layer], y_r.at[layer], dev(mp=(y + d) % NY))
        kv_spread(layer)
        wait(h_buf.at[0:3 * tb2, 0:kw], y0_r.at[layer])
        send(h_buf.at[:, own_cols], h_buf.at[:, own_cols], sb_s.at[layer], sb_r.at[layer], sib)
        wait(h_buf.at[0:3 * tb2, 0:2 * kw], y_r.at[layer])
        wait(h_buf.at[:, 0:kw], sb_r.at[layer])

        def share(j, g):
            blkref = m_buf.at[j, c, g]
            send(blkref, blkref, d_s.at[layer], d_r.at[layer, j], sib)

        def stage_m_out(j, m):
            m_buf[j, c, group] = m
            blkref = m_buf.at[j, c, group]
            send(blkref, blkref, ring_s.at[layer], ring_r.at[layer, j, 0], ring)
            share(j, group)

        def stage_r(j, s):
            g = group_at(s)
            blkref = m_buf.at[j, c, g]
            wait(blkref, ring_r.at[layer, j, s - 1])
            if s < NX - 1:
                send(blkref, blkref, ring_s.at[layer], ring_r.at[layer, j, s], ring)
            share(j, g)

        def stage_d(j):
            wait(m_buf.at[j, 1 - c], d_r.at[layer, j])
            for hf in range(2):
                lhs = jnp.concatenate([m_buf[j, hf, g] for g in range(NX)], axis=1)
                acc[hf * half:(hf + 1) * half, :] += jnp.dot(lhs, wb[j], preferred_element_type=F32)

        def stage_p(j):
            wait(w_ml.at[layer, j], w_r.at[layer, j])
            for n in range(2):
                zs[j, :, n * CW:(n + 1) * CW] = jnp.dot(h_buf[...], w_ml[layer, j, :, n * CW:(n + 1) * CW], preferred_element_type=F32)
            send(zs.at[j, far_rows], zr.at[j], p_s.at[layer, j], p_r.at[layer, j], partner)

        def stage_m(j):
            wait(zr.at[j], p_r.at[layer, j])
            z = zs[j, own_rows, :] + zr[j]
            gate = z[:, 0:CW].astype(BF16).astype(F32)
            up = z[:, CW:2 * CW].astype(BF16).astype(F32)
            stage_m_out(j, (jax.nn.silu(gate) * up).astype(BF16))

        def attn_p():
            wait(w_at.at[layer, 0:(4 * kw * gq + 2 * kw * gkv) // (gq + gkv)], wa_r.at[layer])
            wait(w_at.at[layer, 0:6 * qr, gq:gq + gkv], kvy_r.at[layer])
            za[...] = jnp.dot(h_buf[...], w_at[layer], preferred_element_type=F32)
            send(za.at[far_rows, 0:gq], zar, p_s.at[layer, nch], p_r.at[layer, nch], partner)
            send(za.at[pl.ds(al((1 - c) * half + y * blk, blk), blk), gq:gq + gkv], zkv, kvp_s.at[layer], kvp_r.at[layer], partner)

        yb = pl.ds(al(y * blk, blk), blk)

        def attn_m():
            wait(zkv, kvp_r.at[layer])
            kv_buf[group, yb, :] = (za[pl.ds(al(c * half + y * blk, blk), blk), gq:gq + gkv] + zkv[...]).astype(BF16)
            send(kv_buf.at[group, yb], kv_buf.at[group, yb], kv_s.at[layer], kv_r.at[layer, 0], ring)
            wait(zar, p_r.at[layer, nch])
            q_buf[...] = (za[own_rows, 0:gq] + zar[...]).astype(BF16)

        def attn_r(s):
            g = group_at(s)
            blkref = kv_buf.at[g, yb]
            wait(blkref, kv_r.at[layer, s - 1])
            if s < NX - 1:
                send(blkref, blkref, kv_s.at[layer], kv_r.at[layer, s], ring)
            else:
                for d in range(1, NY):
                    send(kv_buf.at[:, yb], kv_buf.at[:, yb], kvz_s.at[layer], kvz_r.at[layer], dev(mp=(y + d) % NY))

        def attn_core():
            wait(kv_buf.at[0:NX - 1], kvz_r.at[layer])
            outs = []
            for b in range(4):
                rows = slice(b * blk, (b + 1) * blk)
                q = rope(q_buf[rows, :], rows)
                k = rope(jnp.concatenate([kv_buf[0, rows, :], kv_buf[1, rows, :]], axis=1), rows)
                v = jnp.concatenate([kv_buf[2, rows, :], kv_buf[3, rows, :]], axis=1)
                scores = lax.dot_general(q, k, (((1,), (1,)), ((), ())), preferred_element_type=F32) * (gq ** -0.5)
                scores = jnp.where(packs[b, :, 0:blk].astype(F32) > 0.5, scores, -1e30)
                ex = jnp.exp(scores - jnp.max(scores, axis=1, keepdims=True))
                prob = (ex / jnp.sum(ex, axis=1, keepdims=True)).astype(BF16)
                outs.append(jnp.dot(prob, v, preferred_element_type=F32).astype(BF16))
            stage_m_out(nch, jnp.concatenate(outs, axis=0))

        last = nch - 1
        issue_all(layer, ((5, 1), (6, 0), (6, 1)))
        attn_p()
        for j in range(nch):
            stage_p(j)
        pl.when(layer == 0)(tables)
        attn_m()
        for j in range(nch):
            stage_m(j)
        wait(h_buf.at[:, 0:kw], sb_s.at[layer])
        wait(wb, wb_r.at[layer])
        attn_r(1)
        stage_r(0, 1)
        stage_r(1, 1)
        attn_r(2)
        stage_r(2, 1)
        stage_r(3, 1)
        attn_r(3)
        for j in range(4, nch):
            stage_r(j, 1)
        attn_core()
        for j in range(3):
            stage_r(j, 2)
        stage_r(nch, 1)
        for j in range(3, nch):
            stage_r(j, 2)
        stage_r(0, 3)
        stage_r(nch, 2)
        stage_r(1, 3)

        @pl.when(layer < layers - 1)
        def _():
            issue_all(layer + 1, ((0, 0), (0, 1), (1, 0), (1, 1), (2, 0), (2, 1)))

        stage_d(0)
        for j in range(2, nch):
            stage_r(j, 3)
            stage_d(j - 1)
        stage_r(nch, 3)
        stage_d(last)
        stage_d(nch)

        up, dn, op = (y + 1) % NY, (y + NY - 1) % NY, (y + 2) % NY

        def part(block, second):
            return pl.ds(al(block * tb2 + second * blk, blk), blk)

        def to_y(rows, dst, rsem, to):
            send(acc.at[rows], dst, rs_s.at[layer], rsem, dev(mp=to))

        send(acc.at[part(op, 0)], rl_in.at[0], rl_s.at[layer, 0], rl_r.at[layer, 0], dev(mp=up))
        send(acc.at[part(op, 1)], rl_in.at[1], rl_s.at[layer, 1], rl_r.at[layer, 1], dev(mp=dn))
        wait(rl_in.at[0], rl_s.at[layer, 0])
        wait(rl_in.at[1], rl_s.at[layer, 1])
        to_y(part(up, 1), rs_in.at[0, blk:tb2], rs_r.at[layer], up)
        to_y(part(dn, 0), rs_in.at[1, 0:blk], rs_r.at[layer], dn)
        wait(rl_in.at[0], rl_r.at[layer, 0])
        acc[part(up, 0), :] += rl_in[0]
        to_y(part(up, 0), rs_in.at[0, 0:blk], rs_r.at[layer], up)
        wait(rl_in.at[1], rl_r.at[layer, 1])
        acc[part(dn, 1), :] += rl_in[1]
        to_y(part(dn, 1), rs_in.at[1, blk:tb2], rs_r.at[layer], dn)
        wait(rs_in, rs_r.at[layer])
        res[...] = res[...] + (acc[y_rows, :] + rs_in[0] + rs_in[1])

        wait(stat_in.at[layer], st_s.at[layer])
        wait(h_buf.at[0:tb2, 0:2 * kw], h_s.at[layer])
        wait(h_buf.at[0:3 * tb2, 0:kw], y0_s.at[layer])
        wait(h_buf.at[0:3 * tb2, 0:2 * kw], y_s.at[layer])
        for j in range(nch):
            wait(zr.at[j], p_s.at[layer, j])
        wait(zar, p_s.at[layer, nch])
        wait(kv_buf.at[0, 0:3 * blk], kv_s.at[layer])
        wait(kv_buf.at[0:NX - 1], kvz_s.at[layer])
        wait(zkv, kvp_s.at[layer])
        wait(w_at.at[layer, 0:2 * qr, gq:gq + gkv], kvx_s.at[layer])
        wait(w_at.at[layer, 0:6 * qr, gq:gq + gkv], kvy_s.at[layer])
        wait(m_buf.at[:, 0, 0:NX - 1], ring_s.at[layer])
        wait(m_buf.at[:, 0], d_s.at[layer])
        wait(acc.at[0:4 * blk], rs_s.at[layer])
        wait(w_at.at[layer, 0:(3 * kw * gq + kw * gkv) // (gq + gkv)], wa_s.at[layer])
        wait(w_ml.at[layer, :, 0:3 * kw], w_s.at[layer])
        return carry

    lax.fori_loop(0, layers, layer_body, 0)

    swap_start(lambda t: res.at[t * blk:(t + 1) * blk], f_in.at[:, pl.ds(al(c * kw, kw), kw)], f_s, f_r)
    swap_wait(res.at[0:blk], f_s, f_r)
    out_ref[...] = f_in[...]

    @pl.when(jnp.logical_not(pack_own))
    def _():
        wait(pack_ref, ps_s.at[0])

    for d in range(1, NX):
        wait(pack_ref, ps_s.at[d])


def solution(mesh):
    def device_body(x_loc, seg_ids, pos_ids, w_q, w_k, w_v, w_gate, w_up, w_out, w_down, gain):
        blk, width_loc = x_loc.shape
        layers, kw, _ = w_q.shape
        head_dim = w_k.shape[-1]
        gq = w_q.shape[-1] // NX
        gff = w_gate.shape[-1] // NX
        gkv = 2 * head_dim // NX
        nch = gff // CW
        tok, half, tb2 = 8 * blk, 4 * blk, 2 * blk
        kg = 4 * kw
        half_dim = head_dim // 2
        hbm = pl.BlockSpec(memory_space=pl.ANY)
        vmem = pl.BlockSpec(memory_space=pltpu.VMEM)
        dma = pltpu.SemaphoreType.DMA
        return pl.pallas_call(
            functools.partial(kernel, (layers, blk, kw, gq, gkv, gff)),
            out_shape=jax.ShapeDtypeStruct((blk, width_loc), F32),
            in_specs=[vmem] * 4 + [hbm] * 7,
            out_specs=vmem,
            scratch_shapes=[
                pltpu.VMEM((layers, kg, gq + gkv), BF16),
                pltpu.VMEM((layers, nch, kg, 2 * CW), BF16),
                pltpu.VMEM((nch + 1, NX * CW, kw), BF16),
                pltpu.VMEM((nch, tok, 2 * CW), F32),
                pltpu.VMEM((nch, half, 2 * CW), F32),
                pltpu.VMEM((tok, gq + gkv), F32),
                pltpu.VMEM((half, gq), F32),
                pltpu.VMEM((blk, gkv), F32),
                pltpu.VMEM((nch + 1, 2, NX, half, CW), BF16),
                pltpu.VMEM((tok, kg), BF16),
                pltpu.VMEM((tok, kw), F32),
                pltpu.VMEM((tb2, kw), F32),
                pltpu.VMEM((NX, half, gkv), BF16),
                pltpu.VMEM((half, gq), BF16),
                pltpu.VMEM((half, half_dim), F32),
                pltpu.VMEM((half, half_dim), F32),
                pltpu.VMEM((4, blk, 256), BF16),
                pltpu.VMEM((8, tb2), F32),
                pltpu.VMEM((layers, 2 * NX - 1, 8, tb2), F32),
                pltpu.VMEM((2, tb2, kw), F32),
                pltpu.VMEM((2, blk, kw), F32),
                pltpu.VMEM((tb2, kw), BF16),
                pltpu.VMEM((blk, width_loc), F32),
                pltpu.VMEM((blk, 256), BF16),
                pltpu.VMEM((128, 128), jnp.int32),
                dma((2,)), dma((2,)), dma((NX,)), dma(()),
                dma((layers,)), dma((layers,)), dma((layers, nch)), dma((layers,)), dma((layers,)),
                dma((layers, nch + 1)), dma((layers, nch + 1)),
                dma((layers,)), dma((layers, nch + 1, NX - 1)), dma((layers,)), dma((layers, nch + 1)),
                dma((layers,)), dma((layers, NX - 1)), dma((layers,)), dma((layers,)),
                dma((layers,)), dma((layers,)), dma((layers,)), dma((layers,)), dma((layers,)), dma((layers,)),
                dma((layers,)), dma((layers,)), dma((layers,)), dma((layers,)), dma((layers, 2)), dma((layers, 2)),
                dma((2,)), dma((2,)),
            ] + [dma((layers,))] * 8,
            compiler_params=pltpu.CompilerParams(collective_id=0, has_side_effects=True, vmem_limit_bytes=60 * 1024 * 1024),
        )(x_loc, seg_ids[None], pos_ids[None], gain, w_q, w_k, w_v, w_gate, w_up, w_out, w_down)

    col_spec = P(None, PLANE_AXES, "mp")
    kv_spec = P(None, PLANE_AXES, None)
    row_spec = P(None, "mp", PLANE_AXES)
    return jax.shard_map(
        device_body,
        mesh=mesh,
        in_specs=(P(TOKEN_AXES, "mp"), P(TOKEN_AXES), P(TOKEN_AXES), col_spec, kv_spec, kv_spec, col_spec, col_spec, row_spec, row_spec, P(None, None)),
        out_specs=P(TOKEN_AXES, "mp"),
        check_vma=False,
    )
```

time: 331 us -> 296 us (0.89)
  Pallas kernels: 322 us -> 294 us
  other arithmetic: 4.85 us -> 0 us
    pallas_call x1, Pallas kernels: 322 us -> 294 us  [device_body(): pl.pallas_call(functools.partial(kernel, (layers, blk, kw, gq, gkv, gff))...]
where the time goes in v2:
time: 296 us
  Pallas kernels  294 us (99%)
    pallas_call x1, Pallas kernels, device_body(): pl.pallas_call(functools.partial(kernel, (layers, blk, kw, gq, gkv, gff))...  294 us

profile of v2, /device:TPU:103, one launch (start us, length us, event | category | flops | bytes accessed | tf_op | source)
XLA Modules:
  0.0 296.1 jit_solution(7058776537242851600)
XLA Ops:
  0.0 294.5 %shard_map.109 = f32[64,768]{1,0:T(8,128)} custom-call(bf16[64,768]{1,0:T(8,128)(2,1)} %x_ref.1, s32[1,64]{1,0:T(1,128)} %bitcast.2, s32[1,64]{1,0:T(1,128)} %bitcast.3, bf16[2,3072]{1,0:T(2,128)(2,1)} %gain_ref.1, bf16[2,384,1024]{2,1,0:T(8,128)(2,1)} %wq.1, bf16[2,384,256]{2,1,0:T(8,128)(2,1)} %wk.1, bf16[2,384,256]{2,1,0:T(8,128)(2,1)} %wv.1, ...), custom_call_target="tpu_custom_call" | custom-call | tf_op jit(solution)/shard_map/pallas_call | solution.py:441
  294.5 1.6 copy.13

commit v3 on v2

--- a/solution.py
+++ b/solution.py
@@ -74,17 +74,20 @@
     def _():
         pl.semaphore_wait(barrier, peers)
 
+    def swap_send(t, src, dst, ssem, rsem):
+        own = jnp.logical_and(x == y, c == t)
+
+        @pl.when(own)
+        def _():
+            local(src, dst, rsem.at[c])
+
+        @pl.when(jnp.logical_not(own))
+        def _():
+            send(src, dst, ssem.at[t], rsem.at[c], dev(tb=y, ta=t, mp=x))
+
     def swap_start(src_of, dst, ssem, rsem):
         for t in range(2):
-            own = jnp.logical_and(x == y, c == t)
-
-            @pl.when(own)
-            def _():
-                local(src_of(t), dst, rsem.at[c])
-
-            @pl.when(jnp.logical_not(own))
-            def _():
-                send(src_of(t), dst, ssem.at[t], rsem.at[c], dev(tb=y, ta=t, mp=x))
+            swap_send(t, src_of(t), dst, ssem, rsem)
 
     def swap_wait(part, ssem, rsem):
         for t in range(2):
@@ -159,7 +162,7 @@
     pack_ref[:, 0:blk] = jnp.where(allowed, 1.0, 0.0).astype(BF16)
     pack_ref[:, 128:256] = pos_cols.astype(F32).astype(BF16)
 
-    pack_slot = (x % 2) * 2 + c
+    pack_slot = c * 2 + x % 2
     pack_core = x // 2
     pack_own = c == pack_core
 
@@ -196,10 +199,22 @@
 
     own_rows = pl.ds(al(c * half, half), half)
     far_rows = pl.ds(al((1 - c) * half, half), half)
-    y_rows = pl.ds(al(y * tb2, tb2), tb2)
+    yh, yl = y // 2, y % 2
+    sub = half // 2
+
+    def sized(rows):
+        return w_at.at[0, 0:rows]
+
+    def hidden():
+        return h_buf[...].reshape(tok, 4 * kw)
 
     def group_at(s):
         return ((x + NX - s) * (1 - c) + (x + s - 1) * c) % NX
+
+    def group_back(s):
+        return ((x + s) * (1 - c) + (x + 2 * NX - s - 1) * c) % NX
+
+    back = dev(tb=prv)
 
     def issue_all(layer, units):
         for idx, part in units:
@@ -228,53 +243,61 @@
         gain = jnp.where(layer == 0, gains[0:1], gains[1:2])
         normed = (r * lax.rsqrt(mean + NORM_EPS) * gain).astype(BF16)
         own_cols = pl.ds(al((2 + c) * kw, kw), kw)
-        h_buf[y_rows, own_cols] = normed
-        mine = h_buf.at[y_rows, own_cols]
-        far = h_buf.at[y_rows, pl.ds(al(c * kw, kw), kw)]
+        for t in range(2):
+            h_buf[yh, t, yl, :, own_cols] = normed[t * blk:(t + 1) * blk]
+        mine = h_buf.at[yh, :, yl, :, own_cols]
+        far = h_buf.at[yh, :, yl, :, pl.ds(al(c * kw, kw), kw)]
         send(mine, far, h_s.at[layer], h_r.at[layer], dev(tb=right, ta=0))
         send(mine, far, h_s.at[layer], h_r.at[layer], dev(tb=left, ta=1))
         for d in range(1, NY):
             send(mine, mine, y0_s.at[layer], y0_r.at[layer], dev(mp=(y + d) % NY))
-        issue_all(layer, ((4, 0), (4, 1), (5, 0)))
+        issue_all(layer, ((4, 0), (4, 1), (5, 0), (5, 1), (6, 0), (6, 1)))
         acc[...] = jnp.zeros_like(acc)
-        wait(h_buf.at[y_rows, 0:2 * kw], h_r.at[layer])
-        near = h_buf.at[y_rows, 0:2 * kw]
+        near = h_buf.at[yh, :, yl, :, 0:2 * kw]
+        wait(near, h_r.at[layer])
         for d in range(1, NY):
             send(near, near, y_s.at[layer], y_r.at[layer], dev(mp=(y + d) % NY))
         kv_spread(layer)
-        wait(h_buf.at[0:3 * tb2, 0:kw], y0_r.at[layer])
-        send(h_buf.at[:, own_cols], h_buf.at[:, own_cols], sb_s.at[layer], sb_r.at[layer], sib)
-        wait(h_buf.at[0:3 * tb2, 0:2 * kw], y_r.at[layer])
-        wait(h_buf.at[:, 0:kw], sb_r.at[layer])
-
-        def share(j, g):
-            blkref = m_buf.at[j, c, g]
-            send(blkref, blkref, d_s.at[layer], d_r.at[layer, j], sib)
+        wait(sized(3 * tb2), y0_r.at[layer])
+        own_all = h_buf.at[:, :, :, :, own_cols]
+        send(own_all, own_all, sb_s.at[layer], sb_r.at[layer], sib)
+        wait(sized(6 * tb2), y_r.at[layer])
+        wait(sized(tok), sb_r.at[layer])
+
+        def piece(j, g, p):
+            return m_buf.at[j, c, g, p * sub:(p + 1) * sub]
+
+        def share(j, g, p):
+            send(piece(j, g, p), piece(j, g, p), d_s.at[layer], d_r.at[layer, j, p], sib)
 
         def stage_m_out(j, m):
             m_buf[j, c, group] = m
-            blkref = m_buf.at[j, c, group]
-            send(blkref, blkref, ring_s.at[layer], ring_r.at[layer, j, 0], ring)
-            share(j, group)
-
-        def stage_r(j, s):
+            for p in range(2):
+                blkref = piece(j, group, p)
+                send(blkref, blkref, ring_s.at[layer], ring_r.at[layer, j, 0, p], ring)
+                share(j, group, p)
+
+        def stage_r(j, s, p):
             g = group_at(s)
-            blkref = m_buf.at[j, c, g]
-            wait(blkref, ring_r.at[layer, j, s - 1])
+            blkref = piece(j, g, p)
+            wait(blkref, ring_r.at[layer, j, s - 1, p])
             if s < NX - 1:
-                send(blkref, blkref, ring_s.at[layer], ring_r.at[layer, j, s], ring)
-            share(j, g)
-
-        def stage_d(j):
-            wait(m_buf.at[j, 1 - c], d_r.at[layer, j])
+                send(blkref, blkref, ring_s.at[layer], ring_r.at[layer, j, s, p], ring)
+            share(j, g, p)
+
+        def stage_d(j, p):
+            wait(m_buf.at[j, 1 - c, :, p * sub:(p + 1) * sub], d_r.at[layer, j, p])
+            lhs = jnp.concatenate([
+                jnp.concatenate([m_buf[j, hf, g, p * sub:(p + 1) * sub] for g in range(NX)], axis=1) for hf in range(2)
+            ], axis=0)
+            out = jnp.dot(lhs, wb[j], preferred_element_type=F32)
             for hf in range(2):
-                lhs = jnp.concatenate([m_buf[j, hf, g] for g in range(NX)], axis=1)
-                acc[hf * half:(hf + 1) * half, :] += jnp.dot(lhs, wb[j], preferred_element_type=F32)
+                acc[hf * half + p * sub:hf * half + (p + 1) * sub, :] += out[hf * sub:(hf + 1) * sub]
 
         def stage_p(j):
             wait(w_ml.at[layer, j], w_r.at[layer, j])
             for n in range(2):
-                zs[j, :, n * CW:(n + 1) * CW] = jnp.dot(h_buf[...], w_ml[layer, j, :, n * CW:(n + 1) * CW], preferred_element_type=F32)
+                zs[j, :, n * CW:(n + 1) * CW] = jnp.dot(hidden(), w_ml[layer, j, :, n * CW:(n + 1) * CW], preferred_element_type=F32)
             send(zs.at[j, far_rows], zr.at[j], p_s.at[layer, j], p_r.at[layer, j], partner)
 
         def stage_m(j):
@@ -287,7 +310,7 @@
         def attn_p():
             wait(w_at.at[layer, 0:(4 * kw * gq + 2 * kw * gkv) // (gq + gkv)], wa_r.at[layer])
             wait(w_at.at[layer, 0:6 * qr, gq:gq + gkv], kvy_r.at[layer])
-            za[...] = jnp.dot(h_buf[...], w_at[layer], preferred_element_type=F32)
+            za[...] = jnp.dot(hidden(), w_at[layer], preferred_element_type=F32)
             send(za.at[far_rows, 0:gq], zar, p_s.at[layer, nch], p_r.at[layer, nch], partner)
             send(za.at[pl.ds(al((1 - c) * half + y * blk, blk), blk), gq:gq + gkv], zkv, kvp_s.at[layer], kvp_r.at[layer], partner)
 
@@ -296,16 +319,16 @@
         def attn_m():
             wait(zkv, kvp_r.at[layer])
             kv_buf[group, yb, :] = (za[pl.ds(al(c * half + y * blk, blk), blk), gq:gq + gkv] + zkv[...]).astype(BF16)
-            send(kv_buf.at[group, yb], kv_buf.at[group, yb], kv_s.at[layer], kv_r.at[layer, 0], ring)
+            send(kv_buf.at[group, yb], kv_buf.at[group, yb], kv_s.at[layer], kv_r.at[layer, 0], back)
             wait(zar, p_r.at[layer, nch])
             q_buf[...] = (za[own_rows, 0:gq] + zar[...]).astype(BF16)
 
         def attn_r(s):
-            g = group_at(s)
+            g = group_back(s)
             blkref = kv_buf.at[g, yb]
             wait(blkref, kv_r.at[layer, s - 1])
             if s < NX - 1:
-                send(blkref, blkref, kv_s.at[layer], kv_r.at[layer, s], ring)
+                send(blkref, blkref, kv_s.at[layer], kv_r.at[layer, s], back)
             else:
                 for d in range(1, NY):
                     send(kv_buf.at[:, yb], kv_buf.at[:, yb], kvz_s.at[layer], kvz_r.at[layer], dev(mp=(y + d) % NY))
@@ -326,74 +349,98 @@
             stage_m_out(nch, jnp.concatenate(outs, axis=0))
 
         last = nch - 1
-        issue_all(layer, ((5, 1), (6, 0), (6, 1)))
         attn_p()
         for j in range(nch):
             stage_p(j)
         pl.when(layer == 0)(tables)
         attn_m()
-        for j in range(nch):
+        stage_m(0)
+        attn_r(1)
+        stage_m(1)
+        attn_r(2)
+        stage_m(2)
+        attn_r(3)
+        stage_m(3)
+        attn_core()
+        for j in range(4, nch):
             stage_m(j)
-        wait(h_buf.at[:, 0:kw], sb_s.at[layer])
+        wait(sized(tok), sb_s.at[layer])
         wait(wb, wb_r.at[layer])
-        attn_r(1)
-        stage_r(0, 1)
-        stage_r(1, 1)
-        attn_r(2)
-        stage_r(2, 1)
-        stage_r(3, 1)
-        attn_r(3)
-        for j in range(4, nch):
-            stage_r(j, 1)
-        attn_core()
-        for j in range(3):
-            stage_r(j, 2)
-        stage_r(nch, 1)
-        for j in range(3, nch):
-            stage_r(j, 2)
-        stage_r(0, 3)
-        stage_r(nch, 2)
-        stage_r(1, 3)
+        order = (0, 1, 2, 3, nch) + tuple(range(4, nch))
+        up, dn, op = (y + 1) % NY, (y + NY - 1) % NY, (y + 2) % NY
+        hb = blk // 2
+
+        def part(block, p, second, rows):
+            return pl.ds(al((block // 2) * half + p * sub + (block % 2) * blk + second * hb, hb), rows)
+
+        def to_y(rows, dst, p, to):
+            send(acc.at[rows], dst, rs_s.at[layer, p], rs_r.at[layer, p], dev(mp=to))
+
+        def sum_relay(p):
+            send(acc.at[part(op, p, 0, hb)], rl_in.at[p, 0], rl_s.at[layer, p, 0], rl_r.at[layer, p, 0], dev(mp=up))
+            send(acc.at[part(op, p, 1, hb)], rl_in.at[p, 1], rl_s.at[layer, p, 1], rl_r.at[layer, p, 1], dev(mp=dn))
+
+        def sum_direct(p):
+            for i in range(2):
+                wait(rl_in.at[p, i], rl_s.at[layer, p, i])
+            to_y(part(up, p, 1, hb), rs_in.at[p, 0, hb:blk], p, up)
+            to_y(part(dn, p, 0, hb), rs_in.at[p, 1, 0:hb], p, dn)
+
+        def sum_pass(p):
+            wait(rl_in.at[p, 0], rl_r.at[layer, p, 0])
+            acc[part(up, p, 0, hb), :] += rl_in[p, 0]
+            to_y(part(up, p, 0, hb), rs_in.at[p, 0, 0:hb], p, up)
+            wait(rl_in.at[p, 1], rl_r.at[layer, p, 1])
+            acc[part(dn, p, 1, hb), :] += rl_in[p, 1]
+            to_y(part(dn, p, 1, hb), rs_in.at[p, 1, hb:blk], p, dn)
+
+        def sum_end(p):
+            wait(rs_in.at[p], rs_r.at[layer, p])
+            rows = slice(p * blk, (p + 1) * blk)
+            res[rows, :] = res[rows, :] + (acc[part(y, p, 0, blk), :] + rs_in[p, 0] + rs_in[p, 1])
+
+            @pl.when(layer == layers - 1)
+            def _():
+                swap_send(p, res.at[rows], f_in.at[:, pl.ds(al(c * kw, kw), kw)], f_s, f_r)
+
+        for s, p in ((1, 0), (2, 0), (1, 1)):
+            for j in order:
+                stage_r(j, s, p)
+        for i, j in enumerate(order):
+            stage_r(j, 3, 0)
+            if i > 0:
+                stage_d(order[i - 1], 0)
+        stage_d(order[-1], 0)
+        sum_relay(0)
+        for j in order[:2]:
+            stage_r(j, 2, 1)
+        sum_direct(0)
+        for j in order[2:4]:
+            stage_r(j, 2, 1)
+        sum_pass(0)
+        for j in order[4:]:
+            stage_r(j, 2, 1)
 
         @pl.when(layer < layers - 1)
         def _():
             issue_all(layer + 1, ((0, 0), (0, 1), (1, 0), (1, 1), (2, 0), (2, 1)))
 
-        stage_d(0)
-        for j in range(2, nch):
-            stage_r(j, 3)
-            stage_d(j - 1)
-        stage_r(nch, 3)
-        stage_d(last)
-        stage_d(nch)
-
-        up, dn, op = (y + 1) % NY, (y + NY - 1) % NY, (y + 2) % NY
-
-        def part(block, second):
-            return pl.ds(al(block * tb2 + second * blk, blk), blk)
-
-        def to_y(rows, dst, rsem, to):
-            send(acc.at[rows], dst, rs_s.at[layer], rsem, dev(mp=to))
-
-        send(acc.at[part(op, 0)], rl_in.at[0], rl_s.at[layer, 0], rl_r.at[layer, 0], dev(mp=up))
-        send(acc.at[part(op, 1)], rl_in.at[1], rl_s.at[layer, 1], rl_r.at[layer, 1], dev(mp=dn))
-        wait(rl_in.at[0], rl_s.at[layer, 0])
-        wait(rl_in.at[1], rl_s.at[layer, 1])
-        to_y(part(up, 1), rs_in.at[0, blk:tb2], rs_r.at[layer], up)
-        to_y(part(dn, 0), rs_in.at[1, 0:blk], rs_r.at[layer], dn)
-        wait(rl_in.at[0], rl_r.at[layer, 0])
-        acc[part(up, 0), :] += rl_in[0]
-        to_y(part(up, 0), rs_in.at[0, 0:blk], rs_r.at[layer], up)
-        wait(rl_in.at[1], rl_r.at[layer, 1])
-        acc[part(dn, 1), :] += rl_in[1]
-        to_y(part(dn, 1), rs_in.at[1, blk:tb2], rs_r.at[layer], dn)
-        wait(rs_in, rs_r.at[layer])
-        res[...] = res[...] + (acc[y_rows, :] + rs_in[0] + rs_in[1])
+        stage_r(order[0], 3, 1)
+        sum_end(0)
+        for i, j in enumerate(order):
+            if i > 0:
+                stage_r(j, 3, 1)
+                stage_d(order[i - 1], 1)
+        stage_d(order[-1], 1)
+        sum_relay(1)
+        sum_direct(1)
+        sum_pass(1)
+        sum_end(1)
 
         wait(stat_in.at[layer], st_s.at[layer])
-        wait(h_buf.at[0:tb2, 0:2 * kw], h_s.at[layer])
-        wait(h_buf.at[0:3 * tb2, 0:kw], y0_s.at[layer])
-        wait(h_buf.at[0:3 * tb2, 0:2 * kw], y_s.at[layer])
+        wait(sized(2 * tb2), h_s.at[layer])
+        wait(sized(3 * tb2), y0_s.at[layer])
+        wait(sized(6 * tb2), y_s.at[layer])
         for j in range(nch):
             wait(zr.at[j], p_s.at[layer, j])
         wait(zar, p_s.at[layer, nch])
@@ -404,14 +451,14 @@
         wait(w_at.at[layer, 0:6 * qr, gq:gq + gkv], kvy_s.at[layer])
         wait(m_buf.at[:, 0, 0:NX - 1], ring_s.at[layer])
         wait(m_buf.at[:, 0], d_s.at[layer])
-        wait(acc.at[0:4 * blk], rs_s.at[layer])
+        for p in range(2):
+            wait(acc.at[0:2 * blk], rs_s.at[layer, p])
         wait(w_at.at[layer, 0:(3 * kw * gq + kw * gkv) // (gq + gkv)], wa_s.at[layer])
         wait(w_ml.at[layer, :, 0:3 * kw], w_s.at[layer])
         return carry
 
     lax.fori_loop(0, layers, layer_body, 0)
 
-    swap_start(lambda t: res.at[t * blk:(t + 1) * blk], f_in.at[:, pl.ds(al(c * kw, kw), kw)], f_s, f_r)
     swap_wait(res.at[0:blk], f_s, f_r)
     out_ref[...] = f_in[...]
 
@@ -453,7 +500,7 @@
                 pltpu.VMEM((half, gq), F32),
                 pltpu.VMEM((blk, gkv), F32),
                 pltpu.VMEM((nch + 1, 2, NX, half, CW), BF16),
-                pltpu.VMEM((tok, kg), BF16),
+                pltpu.VMEM((2, 2, 2, blk, kg), BF16),
                 pltpu.VMEM((tok, kw), F32),
                 pltpu.VMEM((tb2, kw), F32),
                 pltpu.VMEM((NX, half, gkv), BF16),
@@ -463,8 +510,8 @@
                 pltpu.VMEM((4, blk, 256), BF16),
                 pltpu.VMEM((8, tb2), F32),
                 pltpu.VMEM((layers, 2 * NX - 1, 8, tb2), F32),
-                pltpu.VMEM((2, tb2, kw), F32),
-                pltpu.VMEM((2, blk, kw), F32),
+                pltpu.VMEM((2, 2, blk, kw), F32),
+                pltpu.VMEM((2, 2, blk // 2, kw), F32),
                 pltpu.VMEM((tb2, kw), BF16),
                 pltpu.VMEM((blk, width_loc), F32),
                 pltpu.VMEM((blk, 256), BF16),
@@ -472,10 +519,10 @@
                 dma((2,)), dma((2,)), dma((NX,)), dma(()),
                 dma((layers,)), dma((layers,)), dma((layers, nch)), dma((layers,)), dma((layers,)),
                 dma((layers, nch + 1)), dma((layers, nch + 1)),
-                dma((layers,)), dma((layers, nch + 1, NX - 1)), dma((layers,)), dma((layers, nch + 1)),
+                dma((layers,)), dma((layers, nch + 1, NX - 1, 2)), dma((layers,)), dma((layers, nch + 1, 2)),
                 dma((layers,)), dma((layers, NX - 1)), dma((layers,)), dma((layers,)),
                 dma((layers,)), dma((layers,)), dma((layers,)), dma((layers,)), dma((layers,)), dma((layers,)),
-                dma((layers,)), dma((layers,)), dma((layers,)), dma((layers,)), dma((layers, 2)), dma((layers, 2)),
+                dma((layers,)), dma((layers,)), dma((layers, 2)), dma((layers, 2)), dma((layers, 2, 2)), dma((layers, 2, 2)),
                 dma((2,)), dma((2,)),
             ] + [dma((layers,))] * 8,
             compiler_params=pltpu.CompilerParams(collective_id=0, has_side_effects=True, vmem_limit_bytes=60 * 1024 * 1024),

time: 296 us -> 285 us (0.963)
  Pallas kernels: 294 us -> 284 us
    pallas_call x1, Pallas kernels: 294 us -> 284 us  [device_body(): pl.pallas_call(functools.partial(kernel, (layers, blk, kw, gq, gkv, gff))...]
where the time goes in v3:
time: 285 us
  Pallas kernels  284 us (100%)
    pallas_call x1, Pallas kernels, device_body(): pl.pallas_call(functools.partial(kernel, (layers, blk, kw, gq, gkv, gff))...  284 us

profile of v3, /device:TPU:103, one launch (start us, length us, event | category | flops | bytes accessed | tf_op | source)
XLA Modules:
  0.0 285.3 jit_solution(17074043087615703885)
XLA Ops:
  0.0 283.6 %shard_map.109 = f32[64,768]{1,0:T(8,128)} custom-call(bf16[64,768]{1,0:T(8,128)(2,1)} %x_ref.1, s32[1,64]{1,0:T(1,128)} %bitcast.2, s32[1,64]{1,0:T(1,128)} %bitcast.3, bf16[2,3072]{1,0:T(2,128)(2,1)} %gain_ref.1, bf16[2,384,1024]{2,1,0:T(8,128)(2,1)} %wq.1, bf16[2,384,256]{2,1,0:T(8,128)(2,1)} %wk.1, bf16[2,384,256]{2,1,0:T(8,128)(2,1)} %wv.1, ...), custom_call_target="tpu_custom_call" | custom-call | tf_op jit(solution)/shard_map/pallas_call | solution.py:488
  283.7 1.6 copy.13

commit v4 on v3

--- a/solution.py
+++ b/solution.py
@@ -24,9 +24,10 @@
 
 def kernel(dims, x_ref, seg_ref, pos_ref, gain_ref, wq, wk, wv, wg, wu, wo, wd, out_ref,
            w_at, w_ml, wb, zs, zr, za, zar, zkv, m_buf, h_buf, acc, res, kv_buf, q_buf, cos_t, sin_t, packs,
-           stat_own, stat_in, rs_in, rl_in, x_in, f_in, pack_ref, ids_t,
+           stat_own, stat_in, rs_in, rl_in, x_in, pack_ref, ids_t,
            xs_s, xs_r, ps_s, ps_r, w_s, wa_s, w_r, wa_r, wb_r, p_s, p_r, ring_s, ring_r, d_s, d_r,
-           kv_s, kv_r, h_s, h_r, y_s, y_r, y0_s, y0_r, sb_s, sb_r, st_s, st_r, rs_s, rs_r, rl_s, rl_r, f_s, f_r, kvx_s, kvx_r, kvy_s, kvy_r, kvp_s, kvp_r, kvz_s, kvz_r):
+           kv_s, kv_r, h_s, h_r, y_s, y_r, y0_s, y0_r, sb_s, sb_r, st_s, st_r,
+           rs_s, rs_r, rl_s, rl_r, f_s, f_r, kvx_s, kvx_r, kvy_s, kvy_r, kvp_s, kvp_r, kvz_s, kvz_r):
     layers, blk, kw, gq, gkv, gff = dims
     nch = gff // CW
     tok = 8 * blk
@@ -109,7 +110,7 @@
         for d in range(1, NY):
             for slot in range(2):
                 piece = w_at.at[layer, kv_quarter(slot), gq:gq + gkv]
-                send(piece, piece, kvy_s.at[layer], kvy_r.at[layer], dev(mp=(y + d) % NY))
+                send(piece, piece, kvy_s, kvy_r, dev(mp=(y + d) % NY))
 
     def issue_w(layer, idx, part):
         if part == 0:
@@ -223,8 +224,8 @@
     def layer_body(layer, carry):
         for g in range(NX):
             for j in range(nch):
-                local(wd.at[layer, g * gff + j * CW:g * gff + (j + 1) * CW], wb.at[j, g * CW:(g + 1) * CW], wb_r.at[layer])
-        local(wo.at[layer], wb.at[nch], wb_r.at[layer])
+                local(wd.at[layer, g * gff + j * CW:g * gff + (j + 1) * CW], wb.at[j, g * CW:(g + 1) * CW], wb_r)
+        local(wo.at[layer], wb.at[nch], wb_r)
 
         r = res[...]
         ssum = jnp.sum(r * r, axis=1, keepdims=True)
@@ -232,9 +233,9 @@
         stat_own[...] = stat
         for d in range(1, 2 * NX):
             q = (me_plane + d) % (2 * NX)
-            send(stat_own, stat_in.at[layer, d - 1], st_s.at[layer], st_r.at[layer], dev(tb=q // 2, ta=q % 2))
+            send(stat_own, stat_in.at[layer, d - 1], st_s, st_r, dev(tb=q // 2, ta=q % 2))
         issue_all(layer, ((3, 0), (3, 1)))
-        wait(stat_in.at[layer], st_r.at[layer])
+        wait(stat_in.at[layer], st_r)
         total = stat
         for d in range(2 * NX - 1):
             total = total + stat_in[layer, d]
@@ -247,46 +248,46 @@
             h_buf[yh, t, yl, :, own_cols] = normed[t * blk:(t + 1) * blk]
         mine = h_buf.at[yh, :, yl, :, own_cols]
         far = h_buf.at[yh, :, yl, :, pl.ds(al(c * kw, kw), kw)]
-        send(mine, far, h_s.at[layer], h_r.at[layer], dev(tb=right, ta=0))
-        send(mine, far, h_s.at[layer], h_r.at[layer], dev(tb=left, ta=1))
+        send(mine, far, h_s, h_r, dev(tb=right, ta=0))
+        send(mine, far, h_s, h_r, dev(tb=left, ta=1))
         for d in range(1, NY):
-            send(mine, mine, y0_s.at[layer], y0_r.at[layer], dev(mp=(y + d) % NY))
+            send(mine, mine, y0_s, y0_r, dev(mp=(y + d) % NY))
         issue_all(layer, ((4, 0), (4, 1), (5, 0), (5, 1), (6, 0), (6, 1)))
         acc[...] = jnp.zeros_like(acc)
         near = h_buf.at[yh, :, yl, :, 0:2 * kw]
-        wait(near, h_r.at[layer])
+        wait(near, h_r)
         for d in range(1, NY):
-            send(near, near, y_s.at[layer], y_r.at[layer], dev(mp=(y + d) % NY))
+            send(near, near, y_s, y_r, dev(mp=(y + d) % NY))
         kv_spread(layer)
-        wait(sized(3 * tb2), y0_r.at[layer])
+        wait(sized(3 * tb2), y0_r)
         own_all = h_buf.at[:, :, :, :, own_cols]
-        send(own_all, own_all, sb_s.at[layer], sb_r.at[layer], sib)
-        wait(sized(6 * tb2), y_r.at[layer])
-        wait(sized(tok), sb_r.at[layer])
+        send(own_all, own_all, sb_s, sb_r, sib)
+        wait(sized(6 * tb2), y_r)
+        wait(sized(tok), sb_r)
 
         def piece(j, g, p):
             return m_buf.at[j, c, g, p * sub:(p + 1) * sub]
 
         def share(j, g, p):
-            send(piece(j, g, p), piece(j, g, p), d_s.at[layer], d_r.at[layer, j, p], sib)
+            send(piece(j, g, p), piece(j, g, p), d_s, d_r.at[j, p], sib)
 
         def stage_m_out(j, m):
             m_buf[j, c, group] = m
             for p in range(2):
                 blkref = piece(j, group, p)
-                send(blkref, blkref, ring_s.at[layer], ring_r.at[layer, j, 0, p], ring)
+                send(blkref, blkref, ring_s, ring_r.at[j, 0, p], ring)
                 share(j, group, p)
 
         def stage_r(j, s, p):
             g = group_at(s)
             blkref = piece(j, g, p)
-            wait(blkref, ring_r.at[layer, j, s - 1, p])
+            wait(blkref, ring_r.at[j, s - 1, p])
             if s < NX - 1:
-                send(blkref, blkref, ring_s.at[layer], ring_r.at[layer, j, s, p], ring)
+                send(blkref, blkref, ring_s, ring_r.at[j, s, p], ring)
             share(j, g, p)
 
         def stage_d(j, p):
-            wait(m_buf.at[j, 1 - c, :, p * sub:(p + 1) * sub], d_r.at[layer, j, p])
+            wait(m_buf.at[j, 1 - c, :, p * sub:(p + 1) * sub], d_r.at[j, p])
             lhs = jnp.concatenate([
                 jnp.concatenate([m_buf[j, hf, g, p * sub:(p + 1) * sub] for g in range(NX)], axis=1) for hf in range(2)
             ], axis=0)
@@ -298,10 +299,10 @@
             wait(w_ml.at[layer, j], w_r.at[layer, j])
             for n in range(2):
                 zs[j, :, n * CW:(n + 1) * CW] = jnp.dot(hidden(), w_ml[layer, j, :, n * CW:(n + 1) * CW], preferred_element_type=F32)
-            send(zs.at[j, far_rows], zr.at[j], p_s.at[layer, j], p_r.at[layer, j], partner)
+            send(zs.at[j, far_rows], zr.at[j], p_s.at[j], p_r.at[j], partner)
 
         def stage_m(j):
-            wait(zr.at[j], p_r.at[layer, j])
+            wait(zr.at[j], p_r.at[j])
             z = zs[j, own_rows, :] + zr[j]
             gate = z[:, 0:CW].astype(BF16).astype(F32)
             up = z[:, CW:2 * CW].astype(BF16).astype(F32)
@@ -309,32 +310,32 @@
 
         def attn_p():
             wait(w_at.at[layer, 0:(4 * kw * gq + 2 * kw * gkv) // (gq + gkv)], wa_r.at[layer])
-            wait(w_at.at[layer, 0:6 * qr, gq:gq + gkv], kvy_r.at[layer])
+            wait(w_at.at[layer, 0:6 * qr, gq:gq + gkv], kvy_r)
             za[...] = jnp.dot(hidden(), w_at[layer], preferred_element_type=F32)
-            send(za.at[far_rows, 0:gq], zar, p_s.at[layer, nch], p_r.at[layer, nch], partner)
-            send(za.at[pl.ds(al((1 - c) * half + y * blk, blk), blk), gq:gq + gkv], zkv, kvp_s.at[layer], kvp_r.at[layer], partner)
+            send(za.at[far_rows, 0:gq], zar, p_s.at[nch], p_r.at[nch], partner)
+            send(za.at[pl.ds(al((1 - c) * half + y * blk, blk), blk), gq:gq + gkv], zkv, kvp_s, kvp_r, partner)
 
         yb = pl.ds(al(y * blk, blk), blk)
 
         def attn_m():
-            wait(zkv, kvp_r.at[layer])
+            wait(zkv, kvp_r)
             kv_buf[group, yb, :] = (za[pl.ds(al(c * half + y * blk, blk), blk), gq:gq + gkv] + zkv[...]).astype(BF16)
-            send(kv_buf.at[group, yb], kv_buf.at[group, yb], kv_s.at[layer], kv_r.at[layer, 0], back)
-            wait(zar, p_r.at[layer, nch])
+            send(kv_buf.at[group, yb], kv_buf.at[group, yb], kv_s, kv_r.at[0], back)
+            wait(zar, p_r.at[nch])
             q_buf[...] = (za[own_rows, 0:gq] + zar[...]).astype(BF16)
 
         def attn_r(s):
             g = group_back(s)
             blkref = kv_buf.at[g, yb]
-            wait(blkref, kv_r.at[layer, s - 1])
+            wait(blkref, kv_r.at[s - 1])
             if s < NX - 1:
-                send(blkref, blkref, kv_s.at[layer], kv_r.at[layer, s], back)
+                send(blkref, blkref, kv_s, kv_r.at[s], back)
             else:
                 for d in range(1, NY):
-                    send(kv_buf.at[:, yb], kv_buf.at[:, yb], kvz_s.at[layer], kvz_r.at[layer], dev(mp=(y + d) % NY))
+                    send(kv_buf.at[:, yb], kv_buf.at[:, yb], kvz_s, kvz_r, dev(mp=(y + d) % NY))
 
         def attn_core():
-            wait(kv_buf.at[0:NX - 1], kvz_r.at[layer])
+            wait(kv_buf.at[0:NX - 1], kvz_r)
             outs = []
             for b in range(4):
                 rows = slice(b * blk, (b + 1) * blk)
@@ -364,8 +365,8 @@
         attn_core()
         for j in range(4, nch):
             stage_m(j)
-        wait(sized(tok), sb_s.at[layer])
-        wait(wb, wb_r.at[layer])
+        wait(sized(tok), sb_s)
+        wait(wb, wb_r)
         order = (0, 1, 2, 3, nch) + tuple(range(4, nch))
         up, dn, op = (y + 1) % NY, (y + NY - 1) % NY, (y + 2) % NY
         hb = blk // 2
@@ -374,34 +375,34 @@
             return pl.ds(al((block // 2) * half + p * sub + (block % 2) * blk + second * hb, hb), rows)
 
         def to_y(rows, dst, p, to):
-            send(acc.at[rows], dst, rs_s.at[layer, p], rs_r.at[layer, p], dev(mp=to))
+            send(acc.at[rows], dst, rs_s.at[p], rs_r.at[p], dev(mp=to))
 
         def sum_relay(p):
-            send(acc.at[part(op, p, 0, hb)], rl_in.at[p, 0], rl_s.at[layer, p, 0], rl_r.at[layer, p, 0], dev(mp=up))
-            send(acc.at[part(op, p, 1, hb)], rl_in.at[p, 1], rl_s.at[layer, p, 1], rl_r.at[layer, p, 1], dev(mp=dn))
+            send(acc.at[part(op, p, 0, hb)], rl_in.at[p, 0], rl_s.at[p, 0], rl_r.at[p, 0], dev(mp=up))
+            send(acc.at[part(op, p, 1, hb)], rl_in.at[p, 1], rl_s.at[p, 1], rl_r.at[p, 1], dev(mp=dn))
 
         def sum_direct(p):
             for i in range(2):
-                wait(rl_in.at[p, i], rl_s.at[layer, p, i])
+                wait(rl_in.at[p, i], rl_s.at[p, i])
             to_y(part(up, p, 1, hb), rs_in.at[p, 0, hb:blk], p, up)
             to_y(part(dn, p, 0, hb), rs_in.at[p, 1, 0:hb], p, dn)
 
         def sum_pass(p):
-            wait(rl_in.at[p, 0], rl_r.at[layer, p, 0])
+            wait(rl_in.at[p, 0], rl_r.at[p, 0])
             acc[part(up, p, 0, hb), :] += rl_in[p, 0]
             to_y(part(up, p, 0, hb), rs_in.at[p, 0, 0:hb], p, up)
-            wait(rl_in.at[p, 1], rl_r.at[layer, p, 1])
+            wait(rl_in.at[p, 1], rl_r.at[p, 1])
             acc[part(dn, p, 1, hb), :] += rl_in[p, 1]
             to_y(part(dn, p, 1, hb), rs_in.at[p, 1, hb:blk], p, dn)
 
         def sum_end(p):
-            wait(rs_in.at[p], rs_r.at[layer, p])
+            wait(rs_in.at[p], rs_r.at[p])
             rows = slice(p * blk, (p + 1) * blk)
             res[rows, :] = res[rows, :] + (acc[part(y, p, 0, blk), :] + rs_in[p, 0] + rs_in[p, 1])
 
             @pl.when(layer == layers - 1)
             def _():
-                swap_send(p, res.at[rows], f_in.at[:, pl.ds(al(c * kw, kw), kw)], f_s, f_r)
+                swap_send(p, res.at[rows], out_ref.at[:, pl.ds(al(c * kw, kw), kw)], f_s, f_r)
 
         for s, p in ((1, 0), (2, 0), (1, 1)):
             for j in order:
@@ -412,47 +413,44 @@
                 stage_d(order[i - 1], 0)
         stage_d(order[-1], 0)
         sum_relay(0)
-        for j in order[:2]:
-            stage_r(j, 2, 1)
-        sum_direct(0)
-        for j in order[2:4]:
-            stage_r(j, 2, 1)
-        sum_pass(0)
-        for j in order[4:]:
+        for j in order:
             stage_r(j, 2, 1)
 
         @pl.when(layer < layers - 1)
         def _():
             issue_all(layer + 1, ((0, 0), (0, 1), (1, 0), (1, 1), (2, 0), (2, 1)))
 
+        sum_direct(0)
         stage_r(order[0], 3, 1)
-        sum_end(0)
-        for i, j in enumerate(order):
-            if i > 0:
-                stage_r(j, 3, 1)
-                stage_d(order[i - 1], 1)
+        for i, j in enumerate(order[1:]):
+            stage_r(j, 3, 1)
+            stage_d(order[i], 1)
+            if i == 0:
+                sum_pass(0)
+            if i == 3:
+                sum_end(0)
         stage_d(order[-1], 1)
         sum_relay(1)
         sum_direct(1)
         sum_pass(1)
         sum_end(1)
 
-        wait(stat_in.at[layer], st_s.at[layer])
-        wait(sized(2 * tb2), h_s.at[layer])
-        wait(sized(3 * tb2), y0_s.at[layer])
-        wait(sized(6 * tb2), y_s.at[layer])
+        wait(stat_in.at[layer], st_s)
+        wait(sized(2 * tb2), h_s)
+        wait(sized(3 * tb2), y0_s)
+        wait(sized(6 * tb2), y_s)
         for j in range(nch):
-            wait(zr.at[j], p_s.at[layer, j])
-        wait(zar, p_s.at[layer, nch])
-        wait(kv_buf.at[0, 0:3 * blk], kv_s.at[layer])
-        wait(kv_buf.at[0:NX - 1], kvz_s.at[layer])
-        wait(zkv, kvp_s.at[layer])
+            wait(zr.at[j], p_s.at[j])
+        wait(zar, p_s.at[nch])
+        wait(kv_buf.at[0, 0:3 * blk], kv_s)
+        wait(kv_buf.at[0:NX - 1], kvz_s)
+        wait(zkv, kvp_s)
         wait(w_at.at[layer, 0:2 * qr, gq:gq + gkv], kvx_s.at[layer])
-        wait(w_at.at[layer, 0:6 * qr, gq:gq + gkv], kvy_s.at[layer])
-        wait(m_buf.at[:, 0, 0:NX - 1], ring_s.at[layer])
-        wait(m_buf.at[:, 0], d_s.at[layer])
+        wait(w_at.at[layer, 0:6 * qr, gq:gq + gkv], kvy_s)
+        wait(m_buf.at[:, 0, 0:NX - 1], ring_s)
+        wait(m_buf.at[:, 0], d_s)
         for p in range(2):
-            wait(acc.at[0:2 * blk], rs_s.at[layer, p])
+            wait(acc.at[0:2 * blk], rs_s.at[p])
         wait(w_at.at[layer, 0:(3 * kw * gq + kw * gkv) // (gq + gkv)], wa_s.at[layer])
         wait(w_ml.at[layer, :, 0:3 * kw], w_s.at[layer])
         return carry
@@ -460,7 +458,6 @@
     lax.fori_loop(0, layers, layer_body, 0)
 
     swap_wait(res.at[0:blk], f_s, f_r)
-    out_ref[...] = f_in[...]
 
     @pl.when(jnp.logical_not(pack_own))
     def _():
@@ -489,7 +486,7 @@
             functools.partial(kernel, (layers, blk, kw, gq, gkv, gff)),
             out_shape=jax.ShapeDtypeStruct((blk, width_loc), F32),
             in_specs=[vmem] * 4 + [hbm] * 7,
-            out_specs=vmem,
+            out_specs=hbm,
             scratch_shapes=[
                 pltpu.VMEM((layers, kg, gq + gkv), BF16),
                 pltpu.VMEM((layers, nch, kg, 2 * CW), BF16),
@@ -513,18 +510,16 @@
                 pltpu.VMEM((2, 2, blk, kw), F32),
                 pltpu.VMEM((2, 2, blk // 2, kw), F32),
                 pltpu.VMEM((tb2, kw), BF16),
-                pltpu.VMEM((blk, width_loc), F32),
                 pltpu.VMEM((blk, 256), BF16),
                 pltpu.VMEM((128, 128), jnp.int32),
                 dma((2,)), dma((2,)), dma((NX,)), dma(()),
-                dma((layers,)), dma((layers,)), dma((layers, nch)), dma((layers,)), dma((layers,)),
-                dma((layers, nch + 1)), dma((layers, nch + 1)),
-                dma((layers,)), dma((layers, nch + 1, NX - 1, 2)), dma((layers,)), dma((layers, nch + 1, 2)),
-                dma((layers,)), dma((layers, NX - 1)), dma((layers,)), dma((layers,)),
-                dma((layers,)), dma((layers,)), dma((layers,)), dma((layers,)), dma((layers,)), dma((layers,)),
-                dma((layers,)), dma((layers,)), dma((layers, 2)), dma((layers, 2)), dma((layers, 2, 2)), dma((layers, 2, 2)),
-                dma((2,)), dma((2,)),
-            ] + [dma((layers,))] * 8,
+                dma((layers,)), dma((layers,)), dma((layers, nch)), dma((layers,)), dma(()),
+                dma((nch + 1,)), dma((nch + 1,)),
+                dma(()), dma((nch + 1, NX - 1, 2)), dma(()), dma((nch + 1, 2)),
+                dma(()), dma((NX - 1,)),
+            ] + [dma(())] * 10 + [
+                dma((2,)), dma((2,)), dma((2, 2)), dma((2, 2)), dma((2,)), dma((2,)), dma((layers,)), dma((layers,)),
+            ] + [dma(())] * 6,
             compiler_params=pltpu.CompilerParams(collective_id=0, has_side_effects=True, vmem_limit_bytes=60 * 1024 * 1024),
         )(x_loc, seg_ids[None], pos_ids[None], gain, w_q, w_k, w_v, w_gate, w_up, w_out, w_down)
 

time: 285 us -> 284 us (level)
  no operation moved by 1% of the time
where the time goes in v4:
time: 284 us
  Pallas kernels  282 us (99%)
    pallas_call x1, Pallas kernels, device_body(): pl.pallas_call(functools.partial(kernel, (layers, blk, kw, gq, gkv, gff))...  282 us

profile of v4, /device:TPU:103, one launch (start us, length us, event | category | flops | bytes accessed | tf_op | source)
XLA Modules:
  0.0 283.5 jit_solution(1979905601519246051)
XLA Ops:
  0.0 281.9 %shard_map.109 = f32[64,768]{1,0:T(8,128)} custom-call(bf16[64,768]{1,0:T(8,128)(2,1)} %x_ref.1, s32[1,64]{1,0:T(1,128)} %bitcast.2, s32[1,64]{1,0:T(1,128)} %bitcast.3, bf16[2,3072]{1,0:T(2,128)(2,1)} %gain_ref.1, bf16[2,384,1024]{2,1,0:T(8,128)(2,1)} %wq.1, bf16[2,384,256]{2,1,0:T(8,128)(2,1)} %wk.1, bf16[2,384,256]{2,1,0:T(8,128)(2,1)} %wv.1, ...), custom_call_target="tpu_custom_call" | custom-call | tf_op jit(solution)/shard_map/pallas_call | solution.py:485
  281.9 1.6 copy.13

commit v5 on v4

--- a/solution.py
+++ b/solution.py
@@ -22,12 +22,12 @@
     return pl.multiple_of(index, unit)
 
 
-def kernel(dims, x_ref, seg_ref, pos_ref, gain_ref, wq, wk, wv, wg, wu, wo, wd, out_ref,
+def kernel(dims, x_ref, seg_hbm, pos_hbm, gain_hbm, wq, wk, wv, wg, wu, wo, wd, out_ref,
            w_at, w_ml, wb, zs, zr, za, zar, zkv, m_buf, h_buf, acc, res, kv_buf, q_buf, cos_t, sin_t, packs,
-           stat_own, stat_in, rs_in, rl_in, x_in, pack_ref, ids_t,
+           stat_own, stat_in, rs_in, rl_in, x_in, pack_ref, ids_t, seg_ref, pos_ref, gain_ref,
            xs_s, xs_r, ps_s, ps_r, w_s, wa_s, w_r, wa_r, wb_r, p_s, p_r, ring_s, ring_r, d_s, d_r,
            kv_s, kv_r, h_s, h_r, y_s, y_r, y0_s, y0_r, sb_s, sb_r, st_s, st_r,
-           rs_s, rs_r, rl_s, rl_r, f_s, f_r, kvx_s, kvx_r, kvy_s, kvy_r, kvp_s, kvp_r, kvz_s, kvz_r):
+           rs_s, rs_r, rl_s, rl_r, f_s, f_r, kvx_s, kvx_r, kvy_s, kvy_r, kvp_s, kvp_r, kvz_s, kvz_r, in_r):
     layers, blk, kw, gq, gkv, gff = dims
     nch = gff // CW
     tok = 8 * blk
@@ -55,6 +55,9 @@
     def wait(ref, sem):
         pltpu.make_async_copy(ref, ref, sem).wait()
 
+    small = ((seg_hbm, seg_ref), (pos_hbm, pos_ref), (gain_hbm, gain_ref))
+    for i, (src, dst) in enumerate(small):
+        local(src, dst, in_r.at[i])
     me_plane = 2 * x + c
     barrier = pltpu.get_barrier_semaphore()
     for d in range(1, 2 * NX):
@@ -153,6 +156,8 @@
     issue_w(0, 0, 0)
     issue_w(0, 0, 1)
 
+    for i, (_, dst) in enumerate(small):
+        wait(dst, in_r.at[i])
     ids_t[...] = jnp.zeros_like(ids_t)
     ids_t[:, 0:blk] = jnp.broadcast_to(seg_ref[...], (128, blk))
     seg_rows, seg_cols = ids_t[0:blk, 0:blk], ids_t[...].T[0:blk, 0:blk]
@@ -369,40 +374,55 @@
         wait(wb, wb_r)
         order = (0, 1, 2, 3, nch) + tuple(range(4, nch))
         up, dn, op = (y + 1) % NY, (y + NY - 1) % NY, (y + 2) % NY
-        hb = blk // 2
-
-        def part(block, p, second, rows):
-            return pl.ds(al((block // 2) * half + p * sub + (block % 2) * blk + second * hb, hb), rows)
-
-        def to_y(rows, dst, p, to):
-            send(acc.at[rows], dst, rs_s.at[p], rs_r.at[p], dev(mp=to))
-
-        def sum_relay(p):
-            send(acc.at[part(op, p, 0, hb)], rl_in.at[p, 0], rl_s.at[p, 0], rl_r.at[p, 0], dev(mp=up))
-            send(acc.at[part(op, p, 1, hb)], rl_in.at[p, 1], rl_s.at[p, 1], rl_r.at[p, 1], dev(mp=dn))
-
-        def sum_direct(p):
+        cuts = ((0, 0, blk), (1, 0, blk // 2), (1, blk // 2, blk // 2))
+
+        def part(block, k, second, rows):
+            p, off, size = cuts[k]
+            return pl.ds(al((block // 2) * half + p * sub + (block % 2) * blk + off + second * (size // 2), size // 2), rows)
+
+        def span(k, second=None):
+            p, off, size = cuts[k]
+            first = p * blk + off
+            if second is None:
+                return slice(first, first + size)
+            return slice(first + second * size // 2, first + (second + 1) * size // 2)
+
+        def relay_span(k):
+            p, off, size = cuts[k]
+            return slice((p * blk + off) // 2, (p * blk + off + size) // 2)
+
+        def to_y(rows, dst, k, to):
+            send(acc.at[rows], dst, rs_s.at[k], rs_r.at[k], dev(mp=to))
+
+        def sum_relay(k):
+            hb = cuts[k][2] // 2
+            send(acc.at[part(op, k, 0, hb)], rl_in.at[0, relay_span(k)], rl_s.at[k, 0], rl_r.at[k, 0], dev(mp=up))
+            send(acc.at[part(op, k, 1, hb)], rl_in.at[1, relay_span(k)], rl_s.at[k, 1], rl_r.at[k, 1], dev(mp=dn))
+
+        def sum_direct(k):
+            hb = cuts[k][2] // 2
             for i in range(2):
-                wait(rl_in.at[p, i], rl_s.at[p, i])
-            to_y(part(up, p, 1, hb), rs_in.at[p, 0, hb:blk], p, up)
-            to_y(part(dn, p, 0, hb), rs_in.at[p, 1, 0:hb], p, dn)
-
-        def sum_pass(p):
-            wait(rl_in.at[p, 0], rl_r.at[p, 0])
-            acc[part(up, p, 0, hb), :] += rl_in[p, 0]
-            to_y(part(up, p, 0, hb), rs_in.at[p, 0, 0:hb], p, up)
-            wait(rl_in.at[p, 1], rl_r.at[p, 1])
-            acc[part(dn, p, 1, hb), :] += rl_in[p, 1]
-            to_y(part(dn, p, 1, hb), rs_in.at[p, 1, hb:blk], p, dn)
-
-        def sum_end(p):
-            wait(rs_in.at[p], rs_r.at[p])
-            rows = slice(p * blk, (p + 1) * blk)
-            res[rows, :] = res[rows, :] + (acc[part(y, p, 0, blk), :] + rs_in[p, 0] + rs_in[p, 1])
+                wait(rl_in.at[i, relay_span(k)], rl_s.at[k, i])
+            to_y(part(up, k, 1, hb), rs_in.at[0, span(k, 1)], k, up)
+            to_y(part(dn, k, 0, hb), rs_in.at[1, span(k, 0)], k, dn)
+
+        def sum_pass(k):
+            hb = cuts[k][2] // 2
+            wait(rl_in.at[0, relay_span(k)], rl_r.at[k, 0])
+            acc[part(up, k, 0, hb), :] += rl_in[0, relay_span(k)]
+            to_y(part(up, k, 0, hb), rs_in.at[0, span(k, 0)], k, up)
+            wait(rl_in.at[1, relay_span(k)], rl_r.at[k, 1])
+            acc[part(dn, k, 1, hb), :] += rl_in[1, relay_span(k)]
+            to_y(part(dn, k, 1, hb), rs_in.at[1, span(k, 1)], k, dn)
+
+        def sum_end(k):
+            p, off, size = cuts[k]
+            wait(rs_in.at[0:2, span(k)], rs_r.at[k])
+            res[span(k), :] = res[span(k), :] + (acc[part(y, k, 0, size), :] + rs_in[0, span(k)] + rs_in[1, span(k)])
 
             @pl.when(layer == layers - 1)
             def _():
-                swap_send(p, res.at[rows], out_ref.at[:, pl.ds(al(c * kw, kw), kw)], f_s, f_r)
+                swap_send(p, res.at[span(k)], out_ref.at[off:off + size, pl.ds(al(c * kw, kw), kw)], f_s, f_r)
 
         for s, p in ((1, 0), (2, 0), (1, 1)):
             for j in order:
@@ -430,10 +450,9 @@
             if i == 3:
                 sum_end(0)
         stage_d(order[-1], 1)
-        sum_relay(1)
-        sum_direct(1)
-        sum_pass(1)
-        sum_end(1)
+        for step in (sum_relay, sum_direct, sum_pass, sum_end):
+            for k in (1, 2):
+                step(k)
 
         wait(stat_in.at[layer], st_s)
         wait(sized(2 * tb2), h_s)
@@ -449,8 +468,8 @@
         wait(w_at.at[layer, 0:6 * qr, gq:gq + gkv], kvy_s)
         wait(m_buf.at[:, 0, 0:NX - 1], ring_s)
         wait(m_buf.at[:, 0], d_s)
-        for p in range(2):
-            wait(acc.at[0:2 * blk], rs_s.at[p])
+        for k in range(3):
+            wait(acc.at[0:2 * cuts[k][2]], rs_s.at[k])
         wait(w_at.at[layer, 0:(3 * kw * gq + kw * gkv) // (gq + gkv)], wa_s.at[layer])
         wait(w_ml.at[layer, :, 0:3 * kw], w_s.at[layer])
         return carry
@@ -480,12 +499,11 @@
         kg = 4 * kw
         half_dim = head_dim // 2
         hbm = pl.BlockSpec(memory_space=pl.ANY)
-        vmem = pl.BlockSpec(memory_space=pltpu.VMEM)
         dma = pltpu.SemaphoreType.DMA
         return pl.pallas_call(
             functools.partial(kernel, (layers, blk, kw, gq, gkv, gff)),
             out_shape=jax.ShapeDtypeStruct((blk, width_loc), F32),
-            in_specs=[vmem] * 4 + [hbm] * 7,
+            in_specs=[hbm] * 11,
             out_specs=hbm,
             scratch_shapes=[
                 pltpu.VMEM((layers, kg, gq + gkv), BF16),
@@ -507,19 +525,22 @@
                 pltpu.VMEM((4, blk, 256), BF16),
                 pltpu.VMEM((8, tb2), F32),
                 pltpu.VMEM((layers, 2 * NX - 1, 8, tb2), F32),
-                pltpu.VMEM((2, 2, blk, kw), F32),
-                pltpu.VMEM((2, 2, blk // 2, kw), F32),
+                pltpu.VMEM((2, tb2, kw), F32),
+                pltpu.VMEM((2, blk, kw), F32),
                 pltpu.VMEM((tb2, kw), BF16),
                 pltpu.VMEM((blk, 256), BF16),
                 pltpu.VMEM((128, 128), jnp.int32),
+                pltpu.VMEM((1, blk), jnp.int32),
+                pltpu.VMEM((1, blk), jnp.int32),
+                pltpu.VMEM(gain.shape, BF16),
                 dma((2,)), dma((2,)), dma((NX,)), dma(()),
                 dma((layers,)), dma((layers,)), dma((layers, nch)), dma((layers,)), dma(()),
                 dma((nch + 1,)), dma((nch + 1,)),
                 dma(()), dma((nch + 1, NX - 1, 2)), dma(()), dma((nch + 1, 2)),
                 dma(()), dma((NX - 1,)),
             ] + [dma(())] * 10 + [
-                dma((2,)), dma((2,)), dma((2, 2)), dma((2, 2)), dma((2,)), dma((2,)), dma((layers,)), dma((layers,)),
-            ] + [dma(())] * 6,
+                dma((3,)), dma((3,)), dma((3, 2)), dma((3, 2)), dma((2,)), dma((2,)), dma((layers,)), dma((layers,)),
+            ] + [dma(())] * 6 + [dma((3,))],
             compiler_params=pltpu.CompilerParams(collective_id=0, has_side_effects=True, vmem_limit_bytes=60 * 1024 * 1024),
         )(x_loc, seg_ids[None], pos_ids[None], gain, w_q, w_k, w_v, w_gate, w_up, w_out, w_down)
 

time: 284 us -> 282 us (level)
  no operation moved by 1% of the time
where the time goes in v5:
time: 282 us
  Pallas kernels  281 us (100%)
    pallas_call x1, Pallas kernels, device_body(): pl.pallas_call(functools.partial(kernel, (layers, blk, kw, gq, gkv, gff))...  281 us

profile of v5, /device:TPU:103, one launch (start us, length us, event | category | flops | bytes accessed | tf_op | source)
XLA Modules:
  0.0 282.2 jit_solution(18073901702078287995)
XLA Ops:
  0.0 280.6 %shard_map.109 = f32[64,768]{1,0:T(8,128)} custom-call(bf16[64,768]{1,0:T(8,128)(2,1)} %x_ref.1, s32[1,64]{1,0:T(1,128)} %bitcast.2, s32[1,64]{1,0:T(1,128)} %bitcast.3, bf16[2,3072]{1,0:T(2,128)(2,1)} %gain_hbm.1, bf16[2,384,1024]{2,1,0:T(8,128)(2,1)} %wq.1, bf16[2,384,256]{2,1,0:T(8,128)(2,1)} %wk.1, bf16[2,384,256]{2,1,0:T(8,128)(2,1)} %wv.1, ...), custom_call_target="tpu_custom_call" | custom-call | tf_op jit(solution)/shard_map/pallas_call | solution.py:503
  280.6 1.6 copy.13

commit v6 on v5

--- a/solution.py
+++ b/solution.py
@@ -447,12 +447,17 @@
             stage_d(order[i], 1)
             if i == 0:
                 sum_pass(0)
-            if i == 3:
+            if i == 5:
                 sum_end(0)
         stage_d(order[-1], 1)
-        for step in (sum_relay, sum_direct, sum_pass, sum_end):
-            for k in (1, 2):
-                step(k)
+        sum_relay(1)
+        sum_relay(2)
+        sum_direct(1)
+        sum_pass(1)
+        sum_direct(2)
+        sum_pass(2)
+        sum_end(1)
+        sum_end(2)
 
         wait(stat_in.at[layer], st_s)
         wait(sized(2 * tb2), h_s)

time: 282 us -> 282 us (level)
  no operation moved by 1% of the time
where the time goes in v6:
time: 282 us; the launch traced here: 281 us
  Pallas kernels  280 us (99%)
    pallas_call x1, Pallas kernels, device_body(): pl.pallas_call(functools.partial(kernel, (layers, blk, kw, gq, gkv, gff))...  280 us

profile of v6, /device:TPU:103, one launch (start us, length us, event | category | flops | bytes accessed | tf_op | source)
XLA Modules:
  0.0 281.3 jit_solution(10591862113275113049)
XLA Ops:
  0.0 279.7 %shard_map.109 = f32[64,768]{1,0:T(8,128)} custom-call(bf16[64,768]{1,0:T(8,128)(2,1)} %x_ref.1, s32[1,64]{1,0:T(1,128)} %bitcast.2, s32[1,64]{1,0:T(1,128)} %bitcast.3, bf16[2,3072]{1,0:T(2,128)(2,1)} %gain_hbm.1, bf16[2,384,1024]{2,1,0:T(8,128)(2,1)} %wq.1, bf16[2,384,256]{2,1,0:T(8,128)(2,1)} %wk.1, bf16[2,384,256]{2,1,0:T(8,128)(2,1)} %wv.1, ...), custom_call_target="tpu_custom_call" | custom-call | tf_op jit(solution)/shard_map/pallas_call | solution.py:508
  279.7 1.6 copy.13
